TPU v7x, 32 devices: a whole 2x2x4 slice. The times are simulated.
32 devices in a mesh: dp: 2 (over x), tp: 4 (over z), pp: 4 (over y, core).
Axes of the slice: x: 2, y: 2, z: 4, core: 2. Of those that a mesh axis runs over, the one named last changes fastest.
Arguments:
- stage_buf: bfloat16 [4, 64, 512, 512], P('pp', 'dp', 'tp'), parts along dimension 1
- new_mb: bfloat16 [64, 512, 512], P('dp', 'tp'), parts along dimension 0
- positions: int32 [512], replicated
- ln_attn: float32 [4, 2, 512], P('pp')
- ln_mlp: float32 [4, 2, 512], P('pp')
- w_qkv: bfloat16 [4, 8, 3, 64, 512], P('pp', 'tp')
- w_out: bfloat16 [4, 512, 512], P('pp', 'tp')
- w_up: bfloat16 [4, 512, 2048], P('pp', None, 'tp')
- w_down: bfloat16 [4, 2048, 512], P('pp', 'tp')
Outputs:
- output 1: bfloat16 [64, 512, 512], P('dp', 'tp', 'pp'), parts along dimension 0
- output 2: bfloat16 [64, 512, 512], P('dp', 'tp', 'pp'), parts along dimension 0
- output 3: bfloat16 [4, 64, 512, 512], P('pp', 'dp', 'tp'), parts along dimension 1
There are 2 independent parts. A program takes and returns all parts, laid end to end along the dimension named above; an argument that names none is the same for every part.
All inputs are finite; a program needn't handle non-finite values.
Results may differ from a plain program's by a relative error of at most 0.0180202.
Values are sent between devices in bfloat16 or wider.
A program may use at most 1 GiB of HBM per device.

v0:
```python
import jax
import jax.numpy as jnp
from jax import lax
from jax.sharding import PartitionSpec as P

LN_EPS = 1e-5
ROPE_BASE = 10000.0


def rope_tables(positions, head_dim):
    inv_freq = 1.0 / (ROPE_BASE ** (jnp.arange(0, head_dim, 2).astype(jnp.float32) / head_dim))
    angles = positions.astype(jnp.float32)[:, None] * inv_freq[None, :]
    return jnp.cos(angles), jnp.sin(angles)


def layer_norm(x_in, ln_params):
    x_wide = x_in.astype(jnp.float32)
    centered = x_wide - jnp.mean(x_wide, axis=-1, keepdims=True)
    variance = jnp.mean(jnp.square(centered), axis=-1, keepdims=True)
    return (centered * lax.rsqrt(variance + LN_EPS) * ln_params[0] + ln_params[1]).astype(jnp.bfloat16)


def rotate_half(x_in, cos_tab, sin_tab):
    half_dim = x_in.shape[-1] // 2
    x_wide = x_in.astype(jnp.float32)
    first_half = x_wide[..., :half_dim]
    second_half = x_wide[..., half_dim:]
    return jnp.concatenate([first_half * cos_tab - second_half * sin_tab, second_half * cos_tab + first_half * sin_tab], axis=-1).astype(jnp.bfloat16)


def attention_heads(a_norm, w_qkv, cos_tab, sin_tab):
    groups = w_qkv.shape[1] - 2
    head_dim = w_qkv.shape[2]
    seq_len = a_norm.shape[1]
    qkv_proj = jnp.einsum("nsd,kjhd->nskjh", a_norm, w_qkv, preferred_element_type=jnp.float32).astype(jnp.bfloat16)
    queries = rotate_half(qkv_proj[:, :, :, :groups], cos_tab[:, None, None], sin_tab[:, None, None])
    key_rot = rotate_half(qkv_proj[:, :, :, groups], cos_tab[:, None], sin_tab[:, None])
    values = qkv_proj[:, :, :, groups + 1]
    scores = jnp.einsum("nskgh,ntkh->nkgst", queries, key_rot, preferred_element_type=jnp.float32) * head_dim ** -0.5
    causal = jnp.arange(seq_len)[:, None] >= jnp.arange(seq_len)[None, :]
    attn_probs = jax.nn.softmax(jnp.where(causal, scores, -1e30), axis=-1).astype(jnp.bfloat16)
    return jnp.einsum("nkgst,ntkh->nskgh", attn_probs, values, preferred_element_type=jnp.float32).astype(jnp.bfloat16)


def local_layer(x_loc, ln_attn, ln_mlp, w_qkv, w_out, w_up, w_down, cos_tab, sin_tab):
    x_full = lax.all_gather(x_loc, "tp", axis=1, tiled=True)
    attn_heads = attention_heads(layer_norm(x_full, ln_attn), w_qkv, cos_tab, sin_tab)
    kv_local, groups, head_dim = attn_heads.shape[2], attn_heads.shape[3], attn_heads.shape[4]
    attn_part = jnp.einsum("nskgh,kghd->nsd", attn_heads, w_out.reshape(kv_local, groups, head_dim, w_out.shape[-1]), preferred_element_type=jnp.float32)
    hidden = jax.nn.gelu(jnp.einsum("nsd,df->nsf", layer_norm(x_full, ln_mlp), w_up, preferred_element_type=jnp.float32), approximate=False).astype(jnp.bfloat16)
    mlp_part = jnp.einsum("nsf,fd->nsd", hidden, w_down, preferred_element_type=jnp.float32)
    part_sum = (attn_part + mlp_part).astype(jnp.bfloat16)
    reduced = lax.psum_scatter(part_sum, "tp", scatter_dimension=1, tiled=True)
    return (x_loc.astype(jnp.float32) + reduced.astype(jnp.float32)).astype(jnp.bfloat16)


def solution(mesh):
    stages = mesh.shape["pp"]
    shift_pairs = [(src_stage, src_stage + 1) for src_stage in range(stages - 1)]
    act_spec = P("dp", "tp", None)
    buf_spec = P("pp", "dp", "tp", None)
    emit_spec = P("dp", "tp", "pp")
    stack_spec = P("pp", None, None)

    def stage_body(stage_buf, new_mb, positions, ln_attn, ln_mlp, w_qkv, w_out, w_up, w_down):
        stage_idx = lax.axis_index("pp")
        cos_tab, sin_tab = rope_tables(positions, w_qkv.shape[3])

        def layer_here(x_loc):
            return local_layer(x_loc, ln_attn[0], ln_mlp[0], w_qkv[0], w_out[0], w_up[0], w_down[0], cos_tab, sin_tab)

        def emit_last(y_loc):
            masked = jnp.where(stage_idx == stages - 1, y_loc, jnp.zeros_like(y_loc))
            return lax.psum_scatter(masked, "pp", scatter_dimension=2, tiled=True)

        y_one = layer_here(stage_buf[0])
        emit_one = emit_last(y_one)
        shifted = lax.ppermute(y_one, "pp", shift_pairs)
        buf_one = jnp.where(stage_idx == 0, new_mb, shifted)
        y_two = layer_here(buf_one)
        emit_two = emit_last(y_two)
        final_buf = lax.ppermute(y_two, "pp", shift_pairs)
        return emit_one, emit_two, final_buf[None]

    return jax.shard_map(stage_body, mesh=mesh, in_specs=(buf_spec, act_spec, P(None), stack_spec, stack_spec, P("pp", "tp", None, None, None), P("pp", "tp", None), P("pp", None, "tp"), P("pp", "tp", None)), out_specs=(emit_spec, emit_spec, buf_spec), check_vma=False)
```

profile of v0, /device:TPU:1, one launch (start us, length us, event | category | flops | bytes accessed | tf_op | source)
XLA Modules:
  0.0 1842.7 jit_solution(6921770602965898112)
XLA Ops:
  11.2 288.5 %all-gather.6.cloned.1.call-done = bf16[1,32,512,512]{3,2,1,0:T(8,128)(2,1)} async-done(((bf16[1,32,128,512]{3,2,1,0:T(8,128)(2,1)}), bf16[1,32,512,512]{3,2,1,0:T(8,128)(2,1)}) %all-gather.6.cloned.1.call-update) | async-done | bytes 16777232 | tf_op jit(solution)/shard_map/all_gather | solution.py:46
  308.3 10.1 fusion.22
  319.1 11.2 fusion.81
  349.5 26.3 %fusion.2 = (f32[32,2,512]{2,1,0:T(2,128)S(1)}, f32[32,2,512,512]{3,2,1,0:T(8,128)}) fusion(pred[512,512]{0,1:T(8,128)(4,1)S(1)} %iota_compare_fusion, bf16[32,512,2,32]{1,3,2,0:T(8,128)(2,1)} %fusion.118, bf16[32,512,2,32]{1,3,2,0:T(8,128)(2,1)} %fusion.117, bf16[32,512,2,32]{1,3,2,0:T(8,128)(2,1)} %get-tuple-element.21, ...), kind=kOutput, calls=%fused_computation.8 | convolution fusion | flops 2214559744 | bytes 75890688 | tf_op jit(solution)/shard_map/nskgh,ntkh->nkgst/dot_general | solution.py:39
  375.9 21.7 %fusion = f32[32,2,512]{2,1,0:T(2,128)S(1)} fusion(f32[32,2,512,512]{3,2,1,0:T(8,128)} %get-tuple-element.30, f32[32,2,512]{2,1,0:T(2,128)S(1)} %get-tuple-element.29, pred[512,512]{0,1:T(8,128)(4,1)S(1)} %iota_compare_fusion), kind=kLoop, calls=%fused_computation.6 | loop fusion | flops 67076096 | bytes 67633152 | tf_op jit(solution)/shard_map/reduce_sum | solution.py:41
  397.6 30.4 %fusion.221 = bf16[32,512,2,64]{1,3,2,0:T(8,128)(2,1)} fusion(f32[32,2,512]{2,1,0:T(2,128)S(1)} %fusion, f32[32,2,512]{2,1,0:T(2,128)S(1)} %get-tuple-element.29, f32[32,2,512,512]{3,2,1,0:T(8,128)} %get-tuple-element.30, pred[512,512]{0,1:T(8,128)(4,1)S(1)} %iota_compare_fusion, bf16[32,512,2,3,64]{1,4,3,2,0:T(8,128)(2,1)} %fusion.81), kind=kOutput, calls=%fused_computation.138.clone.1 | convolution fusion | flops 2233466880 | bytes 76021760 | tf_op jit(solution)/shard_map/nkgst,ntkh->nskgh/dot_general | solution.py:42
  428.1 25.9 %convert_reduce_fusion.5 = (u32[512,512]{1,0:T(8,128)S(1)}, u32[512,512]{1,0:T(8,128)S(1)}, f32[32,512,512]{2,1,0:T(8,128)}) fusion(bf16[1,512,512]{2,1,0:T(8,128)(2,1)S(1)} %copy-done, bf16[1,32,512,512]{3,2,1,0:T(8,128)(2,1)} %all-gather.6.cloned.1.call-done, f32[512]{0:T(512)S(1)} %bitcast.274, f32[512]{0:T(512)S(1)} %bitcast.272, ...), kind=kOutput, calls=%fused_computation.49 | convolution fusion | flops 8732016640 | bytes 53088256 | tf_op jit(solution)/shard_map/nsd,df->nsf/dot_general | solution.py:50
  453.9 78.8 %fusion.75 = f32[32,512,512]{2,1,0:T(8,128)} fusion(f32[32,512,512]{2,1,0:T(8,128)} %get-tuple-element.28, u32[512,512]{1,0:T(8,128)S(1)} %get-tuple-element.6, u32[512,512]{1,0:T(8,128)S(1)} %get-tuple-element.5, bf16[1,512,512]{2,1,0:T(8,128)(2,1)S(1)} %copy-done.27), kind=kOutput, calls=%fused_computation.107 | convolution fusion | flops 9160359936 | bytes 69730304 | tf_op jit(solution)/shard_map/nsf,fd->nsd/dot_general | solution.py:51
  532.7 18.9 %fusion.32 = bf16[32,512,512]{2,1,0:T(8,128)(2,1)} fusion(f32[32,512,512]{2,1,0:T(8,128)} %fusion.75, bf16[2,64,512,1]{2,1,0,3:T(8,128)(2,1)S(1)} %bitcast.270, bf16[32,512,2,64]{1,3,2,0:T(8,128)(2,1)S(1)} %copy-done.2), kind=kOutput, calls=%fused_computation.55 | convolution fusion | flops 2164260864 | bytes 54657024 | tf_op jit(solution)/shard_map/nskgh,kghd->nsd/dot_general | solution.py:49
  551.7 275.6 %reduce-scatter.9.cloned.1.call-done = bf16[32,128,512]{2,1,0:T(8,128)(2,1)} async-done(((bf16[32,512,512]{2,1,0:T(8,128)(2,1)}), bf16[32,128,512]{2,1,0:T(8,128)(2,1)}) %reduce-scatter.9.cloned.1.call-update) | async-done | bytes 4194320 | tf_op jit(solution)/shard_map/reduce_scatter | solution.py:53
  841.8 45.4 %collective-permute-done = bf16[32,128,512]{2,1,0:T(8,128)(2,1)} collective-permute-done((bf16[32,128,512]{2,1,0:T(8,128)(2,1)}, bf16[32,128,512]{2,1,0:T(8,128)(2,1)}, u32[]{:S(2)}, u32[]{:S(2)}) %collective-permute-start) | collective-permute-done | bytes 4194336 | tf_op jit(solution)/shard_map/ppermute | solution.py:78
  891.8 289.2 %all-gather.4.cloned.1.call-done = bf16[32,512,512]{2,1,0:T(8,128)(2,1)} async-done(((bf16[32,128,512]{2,1,0:T(8,128)(2,1)}), bf16[32,512,512]{2,1,0:T(8,128)(2,1)}) %all-gather.4.cloned.1.call-update) | async-done | bytes 16777232 | tf_op jit(solution)/shard_map/all_gather | solution.py:46
  1189.9 10.1 fusion.12
  1200.8 11.3 fusion.78
  1212.0 11.7 slice_convert_fusion
  1236.9 26.3 %fusion.3 = (f32[32,2,512]{2,1,0:T(2,128)S(1)}, f32[32,2,512,512]{3,2,1,0:T(8,128)}) fusion(pred[512,512]{0,1:T(8,128)(4,1)S(1)} %copy-done.4, bf16[32,512,2,32]{1,3,2,0:T(8,128)(2,1)} %get-tuple-element.17, bf16[32,512,2,32]{1,3,2,0:T(8,128)(2,1)} %get-tuple-element.16, bf16[32,512,2,32]{1,3,2,0:T(8,128)(2,1)} %get-tuple-element.19, ...), kind=kOutput, calls=%fused_computation.9 | convolution fusion | flops 2214559744 | bytes 75890688 | tf_op jit(solution)/shard_map/nskgh,ntkh->nkgst/dot_general | solution.py:39
  1263.2 21.7 %fusion.1 = f32[32,2,512]{2,1,0:T(2,128)S(1)} fusion(f32[32,2,512,512]{3,2,1,0:T(8,128)} %get-tuple-element.33, f32[32,2,512]{2,1,0:T(2,128)S(1)} %get-tuple-element.32, pred[512,512]{0,1:T(8,128)(4,1)S(1)} %copy-done.4), kind=kLoop, calls=%fused_computation.7 | loop fusion | flops 67076096 | bytes 67633152 | tf_op jit(solution)/shard_map/reduce_sum | solution.py:41
  1284.9 30.8 %fusion.218 = bf16[32,512,2,64]{1,3,2,0:T(8,128)(2,1)} fusion(f32[32,2,512]{2,1,0:T(2,128)S(1)} %fusion.1, f32[32,2,512]{2,1,0:T(2,128)S(1)} %get-tuple-element.32, f32[32,2,512,512]{3,2,1,0:T(8,128)} %get-tuple-element.33, pred[512,512]{0,1:T(8,128)(4,1)S(1)} %copy-done.4, bf16[32,512,2,3,64]{1,4,2,0,3:T(8,128)(2,1)} %fusion.78), kind=kOutput, calls=%fused_computation.137.clone.1 | convolution fusion | flops 2233466880 | bytes 76021760 | tf_op jit(solution)/shard_map/nkgst,ntkh->nskgh/dot_general | solution.py:42
  1315.7 25.9 %convert_reduce_fusion.3 = (u32[512,512]{1,0:T(8,128)S(1)}, u32[512,512]{1,0:T(8,128)S(1)}, f32[32,512,512]{2,1,0:T(8,128)}) fusion(bf16[1,512,512]{2,1,0:T(8,128)(2,1)S(1)} %copy-done, bf16[32,512,512]{2,1,0:T(8,128)(2,1)} %all-gather.4.cloned.1.call-done, f32[32,512]{1,0:T(8,128)S(1)} %copy-done.16, f32[32,512]{1,0:T(8,128)S(1)} %copy-done.12, ...), kind=kOutput, calls=%fused_computation.44 | convolution fusion | flops 8732016640 | bytes 53088256 | tf_op jit(solution)/shard_map/nsd,df->nsf/dot_general | solution.py:50
  1341.6 78.7 %fusion.73 = f32[32,512,512]{2,1,0:T(8,128)} fusion(f32[32,512,512]{2,1,0:T(8,128)} %get-tuple-element.31, u32[512,512]{1,0:T(8,128)S(1)} %get-tuple-element.4, u32[512,512]{1,0:T(8,128)S(1)} %get-tuple-element.3, bf16[1,512,512]{2,1,0:T(8,128)(2,1)S(1)} %copy-done.28), kind=kOutput, calls=%fused_computation.106 | convolution fusion | flops 9160359936 | bytes 69730304 | tf_op jit(solution)/shard_map/nsf,fd->nsd/dot_general | solution.py:51
  1420.3 18.9 %fusion.29 = bf16[32,512,512]{2,1,0:T(8,128)(2,1)} fusion(f32[32,512,512]{2,1,0:T(8,128)} %fusion.73, bf16[2,64,512,1]{2,1,0,3:T(8,128)(2,1)S(1)} %bitcast.271, bf16[32,512,2,64]{1,3,2,0:T(8,128)(2,1)S(1)} %copy-done.1), kind=kOutput, calls=%fused_computation.51 | convolution fusion | flops 2164260864 | bytes 54657024 | tf_op jit(solution)/shard_map/nskgh,kghd->nsd/dot_general | solution.py:49
  1455.9 259.0 %reduce-scatter.11.cloned.1.call-done = bf16[32,128,512]{2,1,0:T(8,128)(2,1)} async-done(((bf16[32,512,512]{2,1,0:T(8,128)(2,1)}), bf16[32,128,512]{2,1,0:T(8,128)(2,1)}) %reduce-scatter.11.cloned.1.call-update) | async-done | bytes 4194320 | tf_op jit(solution)/shard_map/reduce_scatter | solution.py:53
  1745.7 21.5 %reduce-scatter.13.cloned.1.call-done = bf16[128,4096]{1,0:T(8,128)(2,1)} async-done(((bf16[512,4096]{1,0:T(8,128)(2,1)}), bf16[128,4096]{1,0:T(8,128)(2,1)}) %reduce-scatter.13.cloned.1.call-update) | async-done | bytes 1048592
  1770.3 57.5 %collective-permute-done.1 = bf16[32,128,512]{2,1,0:T(8,128)(2,1)} collective-permute-done((bf16[32,128,512]{2,1,0:T(8,128)(2,1)}, bf16[32,128,512]{2,1,0:T(8,128)(2,1)}, u32[]{:S(2)}, u32[]{:S(2)}) %collective-permute-start.1) | collective-permute-done | bytes 4194336 | tf_op jit(solution)/shard_map/ppermute | solution.py:82
  (125 shorter events, 132.5 us)
Async XLA Ops:
  7.2 420.9 %copy-start = (bf16[1,512,512]{2,1,0:T(8,128)(2,1)S(1)}, bf16[1,512,512]{2,1,0:T(8,128)(2,1)}, u32[]{:S(2)}) copy-start(bf16[1,512,512]{2,1,0:T(8,128)(2,1)} %param.16) | copy-start | bytes 1572868
  7.2 311.8 %copy-start.29 = (bf16[1,2,3,64,512]{4,3,2,1,0:T(8,128)(2,1)S(1)}, bf16[1,2,3,64,512]{4,3,2,1,0:T(8,128)(2,1)}, u32[]{:S(2)}) copy-start(bf16[1,2,3,64,512]{4,3,2,1,0:T(8,128)(2,1)} %param.14) | copy-start | bytes 1179652
  7.2 292.5 %all-gather.6.cloned.1.call-start = ((), (), s32[]{:S(2)}) async-start(), calls=%async_computation.7 | async-start | bytes 20971520 | tf_op jit(solution)/shard_map/all_gather | solution.py:46
  7.9 819.4 %reduce-scatter.9.cloned.1.call-start = ((), (), s32[]{:S(2)}) async-start(), calls=%async_computation.4 | async-start | bytes 20971520 | tf_op jit(solution)/shard_map/reduce_scatter | solution.py:53
  8.8 388.8 %copy-start.3 = (pred[512,512]{0,1:T(8,128)(4,1)}, pred[512,512]{0,1:T(8,128)(4,1)S(1)}, u32[]{:S(2)}) copy-start(pred[512,512]{0,1:T(8,128)(4,1)S(1)} %iota_compare_fusion) | copy-start | bytes 786436
  9.5 320.7 %copy-start.23 = (f32[1,1,512]{2,1,0:T(1,128)}, f32[1,1,512]{2,1,0:T(1,128)S(1)}, u32[]{:S(2)}) copy-start(f32[1,1,512]{2,1,0:T(1,128)S(1)} %get-tuple-element.22) | copy-start | bytes 6148
  9.6 320.7 %copy-start.25 = (f32[1,1,512]{2,1,0:T(1,128)}, f32[1,1,512]{2,1,0:T(1,128)S(1)}, u32[]{:S(2)}) copy-start(f32[1,1,512]{2,1,0:T(1,128)S(1)} %get-tuple-element.23) | copy-start | bytes 6148
  11.2 335.5 %copy-start.5 = (f32[512,32]{0,1:T(8,128)}, f32[512,32]{0,1:T(8,128)S(1)}, u32[]{:S(2)}) copy-start(f32[512,32]{0,1:T(8,128)S(1)} %get-tuple-element.26) | copy-start | bytes 196612
  11.2 335.4 %copy-start.7 = (f32[512,32]{0,1:T(8,128)}, f32[512,32]{0,1:T(8,128)S(1)}, u32[]{:S(2)}) copy-start(f32[512,32]{0,1:T(8,128)S(1)} %get-tuple-element.27) | copy-start | bytes 196612
  453.9 78.8 %copy-start.2 = (bf16[32,512,2,64]{1,3,2,0:T(8,128)(2,1)S(1)}, bf16[32,512,2,64]{1,3,2,0:T(8,128)(2,1)}, u32[]{:S(2)}) copy-start(bf16[32,512,2,64]{1,3,2,0:T(8,128)(2,1)} %fusion.221) | copy-start | bytes 12582916
  453.9 78.8 %copy-start.9 = (bf16[1,128,512]{2,1,0:T(8,128)(2,1)S(1)}, bf16[1,128,512]{2,1,0:T(8,128)(2,1)}, u32[]{:S(2)}) copy-start(bf16[1,128,512]{2,1,0:T(8,128)(2,1)} %param.15) | copy-start | bytes 393220
  551.7 629.4 %all-gather.4.cloned.1.call-start = ((), (), s32[]{:S(2)}) async-start(), calls=%async_computation.5 | async-start | bytes 20971520 | tf_op jit(solution)/shard_map/all_gather | solution.py:46
  551.7 649.0 %copy-start.24 = (f32[1,1,512]{2,1,0:T(1,128)S(1)}, f32[1,1,512]{2,1,0:T(1,128)}, u32[]{:S(2)}) copy-start(f32[1,1,512]{2,1,0:T(1,128)} %copy-done.23) | copy-start | bytes 6148
  551.7 649.0 %copy-start.26 = (f32[1,1,512]{2,1,0:T(1,128)S(1)}, f32[1,1,512]{2,1,0:T(1,128)}, u32[]{:S(2)}) copy-start(f32[1,1,512]{2,1,0:T(1,128)} %copy-done.25) | copy-start | bytes 6148
  551.7 649.0 %copy-start.30 = (bf16[1,2,3,64,512]{4,3,2,1,0:T(8,128)(2,1)S(1)}, bf16[1,2,3,64,512]{4,3,2,1,0:T(8,128)(2,1)}, u32[]{:S(2)}) copy-start(bf16[1,2,3,64,512]{4,3,2,1,0:T(8,128)(2,1)} %param.14) | copy-start | bytes 1179652
  836.5 50.7 %collective-permute-start = (bf16[32,128,512]{2,1,0:T(8,128)(2,1)}, bf16[32,128,512]{2,1,0:T(8,128)(2,1)}, u32[]{:S(2)}, u32[]{:S(2)}) collective-permute-start(bf16[32,128,512]{2,1,0:T(8,128)(2,1)} %get-tuple-element.10), channel_id=1, source_target_pairs={{0,1},{1,2},{2,3},{4,5},{5,6},{6,7},{8,9},{9,10},{10,11},{12,13},{... | collective-permute-start | bytes 12582920 | tf_op jit(solution)/shard_map/ppermute | solution.py:78
  891.8 823.1 %reduce-scatter.11.cloned.1.call-start = ((), (), s32[]{:S(2)}) async-start(), calls=%async_computation.6 | async-start | bytes 20971520 | tf_op jit(solution)/shard_map/reduce_scatter | solution.py:53
  1284.9 30.8 %copy-start.12 = (f32[32,512]{1,0:T(8,128)S(1)}, f32[32,512]{1,0:T(8,128)}, u32[]{:S(2)}) copy-start(f32[32,512]{1,0:T(8,128)} %copy-done.11) | copy-start | bytes 196612
  1284.9 30.8 %copy-start.16 = (f32[32,512]{1,0:T(8,128)S(1)}, f32[32,512]{1,0:T(8,128)}, u32[]{:S(2)}) copy-start(f32[32,512]{1,0:T(8,128)} %copy-done.15) | copy-start | bytes 196612
  1341.6 78.7 %copy-start.1 = (bf16[32,512,2,64]{1,3,2,0:T(8,128)(2,1)S(1)}, bf16[32,512,2,64]{1,3,2,0:T(8,128)(2,1)}, u32[]{:S(2)}) copy-start(bf16[32,512,2,64]{1,3,2,0:T(8,128)(2,1)} %fusion.218) | copy-start | bytes 12582916
  1341.6 78.7 %copy-start.10 = (bf16[1,128,512]{2,1,0:T(8,128)(2,1)S(1)}, bf16[1,128,512]{2,1,0:T(8,128)(2,1)}, u32[]{:S(2)}) copy-start(bf16[1,128,512]{2,1,0:T(8,128)(2,1)} %param.15) | copy-start | bytes 393220
  1439.3 327.9 %reduce-scatter.13.cloned.1.call-start = ((), (), s32[]{:S(2)}) async-start(), calls=%async_computation.8 | async-start | bytes 5242880
  1455.6 372.2 %reduce-scatter.15.cloned.1.call-start = ((), (), s32[]{:S(2)}) async-start(), calls=%async_computation.9 | async-start | bytes 5242880
  1740.4 87.5 %collective-permute-start.1 = (bf16[32,128,512]{2,1,0:T(8,128)(2,1)}, bf16[32,128,512]{2,1,0:T(8,128)(2,1)}, u32[]{:S(2)}, u32[]{:S(2)}) collective-permute-start(bf16[32,128,512]{2,1,0:T(8,128)(2,1)} %get-tuple-element.8), channel_id=1, source_target_pairs={{0,1},{1,2},{2,3},{4,5},{5,6},{6,7},{8,9},{9,10},{10,11},{12,13},{... | collective-permute-start | bytes 12582920 | tf_op jit(solution)/shard_map/ppermute | solution.py:82
  (23 other events, 448.7 us)
Sparse Core Ops, SparseCore 0:
  9.6 290.1 all-gather.5
  551.8 275.4 reduce-scatter.8
  891.9 289.1 all-gather.3
  1439.4 275.4 reduce-scatter.10
  1717.9 49.2 reduce-scatter.12
  1769.6 56.0 reduce-scatter.14
where the time goes:
time: 1850 us; the launch traced here: 1840 us
  waiting for transfers between devices  1240 us (67%)
  matrix products  383 us (21%)
  other arithmetic  149 us (8%)
  local copies, waits for them, and re-layouts  47.1 us (3%)
    all_gather x2, waiting for transfers between devices, local_layer(): x_full = lax.all_gather(x_loc, 'tp', axis=1, tiled=True)  578 us
    reduce_scatter x2, waiting for transfers between devices, local_layer(): reduced = lax.psum_scatter(part_sum, 'tp', scatter_dimension=1, tiled=True)  535 us
    dot_general x2, matrix products, local_layer(): jnp.einsum('nsf,fd->nsd', hidden, w_down, preferred_element_type=jnp.floa...  157 us
    dot_general x2, matrix products, attention_heads(): jnp.einsum('nkgst,ntkh->nskgh', attn_probs, values, preferred_element_typ...  61.2 us
    ppermute x1, waiting for transfers between devices, stage_body(): final_buf = lax.ppermute(y_two, 'pp', shift_pairs)  57.5 us
    dot_general x2, matrix products, attention_heads(): jnp.einsum('nskgh,ntkh->nkgst', queries, key_rot, preferred_element_type=...  52.7 us
    dot_general x2, matrix products, local_layer(): jnp.einsum('nsd,df->nsf', layer_norm(x_full, ln_mlp), w_up, preferred_ele...  51.7 us
    ppermute x1, waiting for transfers between devices, stage_body(): shifted = lax.ppermute(y_one, 'pp', shift_pairs)  45.4 us
  transfers between devices with their start and end apart: 8, of which 7 were waited for; matrix products, arithmetic and copies ran while one was open for 3% of the time, Pallas kernels for 0%

commit v1 on v0

v1 whole, which is shorter than its diff:
```python
import functools

import jax
import jax.numpy as jnp
from jax import lax
from jax.experimental import pallas as pl
from jax.experimental.pallas import tpu as pltpu
from jax.sharding import PartitionSpec as P

LN_EPS = 1e-5
ROPE_BASE = 10000.0
MESH = pl.DeviceIdType.MESH
NT = (((1,), (1,)), ((), ()))
F32 = jnp.float32
BF16 = jnp.bfloat16


def rope_tables(positions, head_dim):
    inv_freq = 1.0 / (ROPE_BASE ** (jnp.arange(0, head_dim, 2).astype(F32) / head_dim))
    angles = positions.astype(F32)[:, None] * inv_freq[None, :]
    cos_tab, sin_tab = jnp.cos(angles), jnp.sin(angles)
    return jnp.concatenate([cos_tab] * 4, 1), jnp.concatenate([-sin_tab, -sin_tab, sin_tab, sin_tab], 1)


def pack_weights(w_qkv, w_out, w_up, w_down):
    heads, three, head_dim, width = w_qkv.shape
    halves = w_qkv.reshape(heads, three, 2, head_dim // 2, width)
    queries = halves[:, 0].transpose(1, 0, 2, 3).reshape(-1, width)
    keys = halves[:, 1].transpose(1, 0, 2, 3).reshape(-1, width)
    values = w_qkv[:, 2].reshape(-1, width)
    return jnp.concatenate([queries, keys, values, w_out, w_up, w_down], 0)


def layer(x_ref, w_ref, ln_ref, cos_ref, sin_ref, m_scr, q_scr, k_scr, v_scr, o_scr, acc_scr):
    seq, width = x_ref.shape
    half = seq // 2
    lane = lax.broadcasted_iota(jnp.int32, (1, 128), 1)

    def norm_rows(r, carry):
        rows = pl.ds(pl.multiple_of(r * half, half), half)
        x_wide = x_ref[rows, :].astype(F32)
        centered = x_wide - jnp.mean(x_wide, axis=-1, keepdims=True)
        variance = jnp.mean(centered * centered, axis=-1, keepdims=True)
        normed = centered * lax.rsqrt(variance + LN_EPS)
        a_norm = (normed * ln_ref[0:1, :] + ln_ref[1:2, :]).astype(BF16)
        m_scr[rows, :] = (normed * ln_ref[2:3, :] + ln_ref[3:4, :]).astype(BF16)
        cos_tab, sin_tab = cos_ref[rows, :], sin_ref[rows, :]
        for s in range(4):
            qkv = lax.dot_general(a_norm, w_ref[s, 0:384, :], NT, preferred_element_type=F32).astype(BF16)
            q_wide, k_wide = qkv[:, 0:128].astype(F32), qkv[:, 128:256].astype(F32)
            q_scr[s, rows, :] = (q_wide * cos_tab + pltpu.roll(q_wide, 64, 1) * sin_tab).astype(BF16)
            k_scr[s, rows, :] = (k_wide * cos_tab + pltpu.roll(k_wide, 64, 1) * sin_tab).astype(BF16)
            v_scr[s, rows, :] = qkv[:, 256:384]
        return carry

    lax.fori_loop(0, 2, norm_rows, 0)

    def head_pair(s, carry):
        row = lax.broadcasted_iota(jnp.int32, (half, half), 0)
        col = lax.broadcasted_iota(jnp.int32, (half, half), 1)
        causal = row >= col
        outs = [None, None]
        for hh in range(2):
            q_mask = jnp.where((lane // 32) % 2 == hh, 0.125, 0.0).astype(BF16)
            v_mask = jnp.where(lane // 64 == hh, 1.0, 0.0).astype(BF16)
            keys = [k_scr[s, 0:half, :], k_scr[s, half:seq, :]]
            vals = [v_scr[s, 0:half, :] * v_mask, v_scr[s, half:seq, :] * v_mask]
            for qb in range(2):
                q_blk = q_scr[s, qb * half:(qb + 1) * half, :] * q_mask
                scores = [lax.dot_general(q_blk, keys[kb], NT, preferred_element_type=F32) for kb in range(qb + 1)]
                scores[qb] = jnp.where(causal, scores[qb], -1e30)
                peak = functools.reduce(jnp.maximum, [jnp.max(sc, axis=-1, keepdims=True) for sc in scores])
                exps = [jnp.exp(sc - peak) for sc in scores]
                total = functools.reduce(jnp.add, [jnp.sum(e, axis=-1, keepdims=True) for e in exps])
                inv = 1.0 / total
                for kb in range(qb + 1):
                    part = jnp.dot((exps[kb] * inv).astype(BF16), vals[kb], preferred_element_type=F32)
                    outs[qb] = part if outs[qb] is None else outs[qb] + part
        for qb in range(2):
            o_scr[qb * half:(qb + 1) * half, pl.ds(pl.multiple_of(s * 128, 128), 128)] = outs[qb].astype(BF16)
        return carry

    lax.fori_loop(0, 4, head_pair, 0)

    def out_rows(r, carry):
        rows = pl.ds(pl.multiple_of(r * half, half), half)
        w_out = w_ref[:, 384:512, :].reshape(width, width)
        acc_scr[rows, :] = x_ref[rows, :].astype(F32) + jnp.dot(o_scr[rows, :], w_out, preferred_element_type=F32)
        return carry

    lax.fori_loop(0, 2, out_rows, 0)

    def mlp_part(c, carry):
        for r in range(2):
            rows = slice(r * half, (r + 1) * half)
            pre = jnp.dot(m_scr[rows, :], w_ref[c, 512:1024, :], preferred_element_type=F32)
            hidden = (0.5 * pre * (1.0 + lax.erf(pre * 0.7071067811865476))).astype(BF16)
            acc_scr[rows, :] += jnp.dot(hidden, w_ref[c, 1024:1536, :], preferred_element_type=F32)
        return carry

    lax.fori_loop(0, 4, mlp_part, 0)
    x_ref[...] = acc_scr[...].astype(BF16)


def kernel(buf_ref, mb_ref, w_loc, ln_ref, cos_ref, sin_ref, emit_one, emit_two, final,
           w_all, xs, zeros, m_scr, q_scr, k_scr, v_scr, o_scr, acc_scr,
           loc_sem, wloc_sem, xs_send, xs_recv, mb_send, mb_recv, y_recv, wz_send, wz_recv, wx_send, wx_recv,
           y_send, emit_recv, final_recv, zero_sem):
    d, t, p = lax.axis_index("dp"), lax.axis_index("tp"), lax.axis_index("pp")
    emits = (emit_one, emit_two)

    def remote(src, dst, send, recv, dp=None, tp=None, pp=None):
        where = (d if dp is None else dp, t if tp is None else tp, p if pp is None else pp)
        return pltpu.make_async_remote_copy(src, dst, send, recv, device_id=where, device_id_type=MESH)

    def wait_bytes(ref, sem):
        pltpu.make_async_copy(ref, ref, sem).wait()

    def seq_rows(rank):
        return pl.ds(pl.multiple_of(rank * 128, 128), 128)

    def x_copy(i, o):
        to = lax.rem(t + o, 4)
        return remote(buf_ref.at[0, 8 * to + i], xs.at[0, i, seq_rows(t), :], xs_send, xs_recv.at[i, o - 1], tp=to)

    def x_arrived(i, o):
        src = lax.rem(t + 4 - o, 4)
        wait_bytes(xs.at[0, i, seq_rows(src), :], xs_recv.at[i, o - 1])

    def mb_copy(i, o):
        to = lax.rem(t + o, 4)
        return remote(mb_ref.at[8 * to + i], xs.at[1, i, seq_rows(t), :], mb_send, mb_recv.at[i, o - 1], tp=to)

    def mb_arrived(i, o):
        src = lax.rem(t + 4 - o, 4)
        wait_bytes(xs.at[1, i, seq_rows(src), :], mb_recv.at[i, o - 1])

    def x_local(i):
        return pltpu.make_async_copy(buf_ref.at[0, 8 * t + i], xs.at[0, i, seq_rows(t), :], loc_sem.at[0, i])

    def mb_local(i):
        return pltpu.make_async_copy(mb_ref.at[8 * t + i], xs.at[1, i, seq_rows(t), :], loc_sem.at[1, i])

    def send_x(i):
        for o in (2, 1, 3):
            x_copy(i, o).start()

    def half_rows(dp, piece):
        size = 256 * (piece + 1)
        return pl.ds(pl.multiple_of(512 * piece + dp * size, 256), size)

    def w_copy_z(s, piece, to, slot, own):
        rows = half_rows(d, piece)
        src = w_loc.at[rows, :] if own else w_all.at[s, rows, :]
        return remote(src, w_all.at[s, rows, :], wz_send.at[slot, piece], wz_recv.at[s, piece], tp=to)

    def w_copy_x(s, piece):
        rows = half_rows(d, piece)
        return remote(w_all.at[s, rows, :], w_all.at[s, rows, :], wx_send.at[s, piece], wx_recv.at[s, piece], dp=1 - d)

    def relay(action):
        for hop in range(4):
            for piece in range(2):
                right_src, left_src = lax.max(t - hop, 0), lax.min(t + hop, 3)
                from_left, from_right = t >= hop, t + hop <= 3
                if hop:
                    for arrived, s in ((from_left, right_src), (from_right, left_src)):
                        @pl.when(arrived)
                        def _():
                            action("arrive", None, s, piece)
                if hop < 3:
                    @pl.when(jnp.logical_and(from_left, t < 3))
                    def _():
                        action("z", w_copy_z(right_src, piece, lax.min(t + 1, 3), 2 * hop, hop == 0), right_src, piece)

                    @pl.when(jnp.logical_and(from_right, t > 0))
                    def _():
                        action("z", w_copy_z(left_src, piece, lax.max(t - 1, 0), 2 * hop + 1, hop == 0), left_src, piece)
                if hop:
                    for arrived, s in ((from_left, right_src), (from_right, left_src)):
                        @pl.when(arrived)
                        def _():
                            action("x", w_copy_x(s, piece), s, piece)
            yield hop

    def start_or_wait(kind, copy, s, piece):
        if kind == "arrive":
            wait_bytes(w_all.at[s, half_rows(d, piece), :], wz_recv.at[s, piece])
        else:
            copy.start()

    def wait_sent(kind, copy, s, piece):
        if kind != "arrive":
            copy.wait_send()

    own_w = pltpu.make_async_copy(w_loc, w_all.at[t], wloc_sem)
    own_w.start()
    for hop in relay(start_or_wait):
        if hop == 0:
            for i in range(8):
                x_local(i).start()
        send_x(2 * hop)
        send_x(2 * hop + 1)

    @pl.when(p == 0)
    def _():
        def body(i, carry):
            mb_local(i).start()
            for o in (2, 1, 3):
                mb_copy(i, o).start()
            return carry
        lax.fori_loop(0, 8, body, 0)
        zeros[...] = jnp.zeros_like(zeros)

        def zero_body(i, carry):
            pltpu.make_async_copy(zeros, final.at[0, i], zero_sem).start()
            return carry
        lax.fori_loop(0, 32, zero_body, 0)

    own_w.wait()
    for o in (1, 2, 3):
        src = lax.rem(t + 4 - o, 4)
        for piece in range(2):
            wait_bytes(w_all.at[src, half_rows(1 - d, piece), :], wx_recv.at[src, piece])

    def emit_copy(tick, i, o, qq):
        to = lax.rem(t + o, 4)
        q = lax.rem(3 + qq, 4)
        src = xs.at[tick, i, seq_rows(to), seq_rows(q)]
        dst = emits[tick].at[8 * t + i]
        if o == 0 and qq == 0:
            return pltpu.make_async_copy(src, dst, emit_recv.at[tick, 0])
        return remote(src, dst, y_send.at[tick, i], emit_recv.at[tick, o], tp=to, pp=q)

    def tick_body(tick):
        def step(i, carry):
            if tick == 0:
                x_local(i).wait()
                for o in (1, 2, 3):
                    x_arrived(i, o)
            else:
                @pl.when(p == 0)
                def _():
                    mb_local(i).wait()
                    for o in (1, 2, 3):
                        mb_arrived(i, o)

                @pl.when(p > 0)
                def _():
                    wait_bytes(xs.at[1, i], y_recv.at[i])
            layer(xs.at[tick, i], w_all, ln_ref, cos_ref, sin_ref, m_scr, q_scr, k_scr, v_scr, o_scr, acc_scr)

            @pl.when(p < 3)
            def _():
                nxt = lax.min(p + 1, 3)
                if tick == 0:
                    remote(xs.at[0, i], xs.at[1, i], y_send.at[0, i], y_recv.at[i], pp=nxt).start()
                else:
                    for o in (2, 1, 3, 0):
                        to = lax.rem(t + o, 4)
                        remote(xs.at[1, i, seq_rows(to), :], final.at[0, 8 * t + i], y_send.at[1, i], final_recv.at[o],
                               tp=to, pp=nxt).start()

            @pl.when(p == 3)
            def _():
                for o in (2, 1, 3, 0):
                    for qq in (1, 2, 3, 0):
                        emit_copy(tick, i, o, qq).start()
            return carry
        lax.fori_loop(0, 8, step, 0)

    tick_body(0)
    tick_body(1)

    wait_bytes(buf_ref.at[0, 0:24], xs_send)
    for _ in relay(wait_sent):
        pass

    @pl.when(p == 0)
    def _():
        wait_bytes(mb_ref.at[0:24], mb_send)
        wait_bytes(final.at[0], zero_sem)

    @pl.when(p > 0)
    def _():
        for o in range(4):
            src = lax.rem(t + 4 - o, 4)
            wait_bytes(final.at[0, pl.ds(8 * src, 8)], final_recv.at[o])

    for tick in range(2):
        for o in range(4):
            src = lax.rem(t + 4 - o, 4)
            wait_bytes(emits[tick].at[pl.ds(8 * src, 8)], emit_recv.at[tick, o])

        def sent(i, carry):
            @pl.when(p < 3)
            def _():
                wait_bytes(xs.at[tick, i], y_send.at[tick, i])

            @pl.when(p == 3)
            def _():
                wait_bytes(emits[tick].at[0:15], y_send.at[tick, i])
            return carry
        lax.fori_loop(0, 8, sent, 0)


def solution(mesh):
    def body(stage_buf, new_mb, positions, ln_attn, ln_mlp, w_qkv, w_out, w_up, w_down):
        cos_tab, sin_tab = rope_tables(positions, w_qkv.shape[3])
        packed = pack_weights(w_qkv[0], w_out[0], w_up[0], w_down[0])
        ln_rows = jnp.concatenate([ln_attn[0], ln_mlp[0]], 0)
        batch, rows, width = new_mb.shape
        seq = 4 * rows
        emit_shape = jax.ShapeDtypeStruct((batch, rows, width // 4), BF16)
        hbm = pl.BlockSpec(memory_space=pl.ANY)
        vmem = pl.BlockSpec(memory_space=pltpu.VMEM)
        dma = pltpu.SemaphoreType.DMA
        return pl.pallas_call(
            kernel,
            out_shape=(emit_shape, emit_shape, jax.ShapeDtypeStruct(stage_buf.shape, BF16)),
            in_specs=[hbm, hbm, hbm, vmem, vmem, vmem],
            out_specs=(hbm, hbm, hbm),
            scratch_shapes=[
                pltpu.VMEM((4, 1536, width), BF16),
                pltpu.VMEM((2, batch // 4, seq, width), BF16),
                pltpu.VMEM((rows, width), BF16),
                pltpu.VMEM((seq, width), BF16),
                pltpu.VMEM((4, seq, 128), BF16),
                pltpu.VMEM((4, seq, 128), BF16),
                pltpu.VMEM((4, seq, 128), BF16),
                pltpu.VMEM((seq, width), BF16),
                pltpu.VMEM((seq, width), F32),
                dma((2, 8)), dma, dma, dma((8, 3)), dma, dma((8, 3)), dma((8,)),
                dma((6, 2)), dma((4, 2)), dma((4, 2)), dma((4, 2)),
                dma((2, 8)), dma((2, 4)), dma((4,)), dma,
            ],
            compiler_params=pltpu.CompilerParams(has_side_effects=True, vmem_limit_bytes=60 * 1024 * 1024),
            cost_estimate=pl.CostEstimate(flops=60_000_000_000, bytes_accessed=40_000_000, transcendentals=50_000_000),
        )(stage_buf, new_mb, packed, ln_rows, cos_tab, sin_tab)

    act_spec = P("dp", "tp", None)
    buf_spec = P("pp", "dp", "tp", None)
    emit_spec = P("dp", "tp", "pp")
    stack_spec = P("pp", None, None)
    return jax.shard_map(body, mesh=mesh, in_specs=(buf_spec, act_spec, P(None), stack_spec, stack_spec, P("pp", "tp", None, None, None), P("pp", "tp", None), P("pp", None, "tp"), P("pp", "tp", None)), out_specs=(emit_spec, emit_spec, buf_spec), check_vma=False)
```

time: 1850 us -> 349 us (0.19)
  waiting for transfers between devices: 1240 us -> 0 us
  matrix products: 383 us -> 0 us
  Pallas kernels: 0 us -> 329 us
  other arithmetic: 149 us -> 4.25 us
  local copies, waits for them, and re-layouts: 47.1 us -> 11.2 us
    all_gather x2 -> x0, waiting for transfers between devices: 578 us -> none  [local_layer(): x_full = lax.all_gather(x_loc, 'tp', axis=1, tiled=True)]
    reduce_scatter x2 -> x0, waiting for transfers between devices: 535 us -> none  [local_layer(): reduced = lax.psum_scatter(part_sum, 'tp', scatter_dimension=1, tiled=True)]
    dot_general x12 -> x0, matrix products: 383 us -> none  [the longest x2 157 us: local_layer(): jnp.einsum('nsf,fd->nsd', hidden, w_down, preferred_element_type=jnp.floa...]
    pallas_call x0 -> x1, Pallas kernels: none -> 329 us  [body(): pl.pallas_call(kernel, out_shape=(emit_shape, emit_shape, jax.ShapeDtypeS...]
    ppermute x2 -> x0, waiting for transfers between devices: 103 us -> none  [the longest x1 57.5 us: stage_body(): final_buf = lax.ppermute(y_two, 'pp', shift_pairs)]
    reduce_sum x6 -> x0, other arithmetic: 80.8 us -> none  [the longest x2 43.3 us: attention_heads(): jax.nn.softmax(jnp.where(causal, scores, -1e+30), axis=-1)]
    unnamed x87 -> x20, local copies, waits for them, and re-layouts: 44.9 us -> 9.26 us
    select_n x3 -> x0, other arithmetic: 22.9 us -> none  [the longest x2 18.3 us: emit_last(): masked = jnp.where(stage_idx == stages - 1, y_loc, jnp.zeros_like(y_loc))]
  transfers between devices with their start and end apart: 8 -> 0, of which waited for: 7 -> 0; matrix products, arithmetic and copies ran while one was open for 3% -> 0% of each run, Pallas kernels for 0% -> 0%
where the time goes in v1:
time: 349 us; the launch traced here: 345 us
  Pallas kernels  329 us (94%)
  local copies, waits for them, and re-layouts  11.2 us (3%)
  other arithmetic  4.25 us (1%)
    pallas_call x1, Pallas kernels, body(): pl.pallas_call(kernel, out_shape=(emit_shape, emit_shape, jax.ShapeDtypeS...  329 us
    unnamed x20, local copies, waits for them, and re-layouts  9.26 us

profile of v1, /device:TPU:1, one launch (start us, length us, event | category | flops | bytes accessed | tf_op | source)
XLA Modules:
  0.0 345.4 jit_solution(16469157742760143794)
XLA Ops:
  0.6 0.7 convert_element_type.10
  1.3 1.3 pad_maximum_fusion.2.ln_ref
  2.6 0.9 slice.14
  3.5 1.0 fusion.1
  4.6 0.0 copy-start.3
  4.6 0.0 copy-start.1
  4.6 1.0 fusion
  5.6 0.0 copy-start.2
  5.6 1.3 pad_maximum_fusion
  6.9 0.0 copy-done.3
  7.0 0.0 copy-done.1
  7.0 0.0 copy-done.2
  7.1 0.0 copy-start.4
  7.1 1.1 copy-done.4
  8.2 329.2 %shard_map.112 = (bf16[32,128,128]{2,1,0:T(8,128)(2,1)}, bf16[32,128,128]{2,1,0:T(8,128)(2,1)}, bf16[1,32,128,512]{3,2,1,0:T(8,128)(2,1)}) custom-call(bf16[1,32,128,512]{3,2,1,0:T(8,128)(2,1)} %buf_ref.1, bf16[32,128,512]{2,1,0:T(8,128)(2,1)} %mb_ref.1, bf16[1536,512]{1,0:T(8,128)(2,1)} %copy-done.4, f32[4,512]{1,0:T(4,128)} %pad_maximum_fusion.2.ln_ref, ...), custom_call_target="tpu_custom_call" | custom-call | flops 60000002048 | bytes 40000000 | tf_op jit(solution)/shard_map/pallas_call | solution.py:318
  337.4 0.0 copy-start
  337.4 2.4 copy.27
  339.8 0.0 copy-done
  339.8 1.0 copy.28
  340.8 4.6 %copy.29 = bf16[1,32,128,512]{3,2,1,0:T(8,128)(2,1)} copy(bf16[1,32,128,512]{3,2,1,0:T(8,128)(2,1)} %get-tuple-element.15) | data formatting | bytes 8388608
  (9 shorter events, 0.1 us)
Async XLA Ops:
  4.6 2.4 copy-start.3
  4.6 2.4 copy-start.1
  5.6 1.4 copy-start.2
  7.1 1.1 copy-start.4
  337.4 2.4 copy-start

commit v2 on v1

--- a/solution.py
+++ b/solution.py
@@ -19,7 +19,9 @@
     inv_freq = 1.0 / (ROPE_BASE ** (jnp.arange(0, head_dim, 2).astype(F32) / head_dim))
     angles = positions.astype(F32)[:, None] * inv_freq[None, :]
     cos_tab, sin_tab = jnp.cos(angles), jnp.sin(angles)
-    return jnp.concatenate([cos_tab] * 4, 1), jnp.concatenate([-sin_tab, -sin_tab, sin_tab, sin_tab], 1)
+    by_row = jnp.stack([jnp.concatenate([cos_tab] * 4, 1), jnp.concatenate([-sin_tab, -sin_tab, sin_tab, sin_tab], 1)])
+    by_lane = jnp.stack([jnp.concatenate([cos_tab.T] * 2, 0), jnp.concatenate([sin_tab.T] * 2, 0)])
+    return by_row, by_lane
 
 
 def pack_weights(w_qkv, w_out, w_up, w_down):
@@ -28,13 +30,12 @@
     queries = halves[:, 0].transpose(1, 0, 2, 3).reshape(-1, width)
     keys = halves[:, 1].transpose(1, 0, 2, 3).reshape(-1, width)
     values = w_qkv[:, 2].reshape(-1, width)
-    return jnp.concatenate([queries, keys, values, w_out, w_up, w_down], 0)
-
-
-def layer(x_ref, w_ref, ln_ref, cos_ref, sin_ref, m_scr, q_scr, k_scr, v_scr, o_scr, acc_scr):
+    return jnp.concatenate([queries, values, keys, w_out, w_up, w_down], 0)
+
+
+def layer(x_ref, w_ref, ln_ref, row_ref, lane_ref, m_scr, q_scr, k_scr, v_scr, o_scr, acc_scr):
     seq, width = x_ref.shape
     half = seq // 2
-    lane = lax.broadcasted_iota(jnp.int32, (1, 128), 1)
 
     def norm_rows(r, carry):
         rows = pl.ds(pl.multiple_of(r * half, half), half)
@@ -44,40 +45,40 @@
         normed = centered * lax.rsqrt(variance + LN_EPS)
         a_norm = (normed * ln_ref[0:1, :] + ln_ref[1:2, :]).astype(BF16)
         m_scr[rows, :] = (normed * ln_ref[2:3, :] + ln_ref[3:4, :]).astype(BF16)
-        cos_tab, sin_tab = cos_ref[rows, :], sin_ref[rows, :]
+        w_k = w_ref[:, 256:384, :].reshape(width, width)
+        keys = lax.dot_general(a_norm, w_k, NT, preferred_element_type=F32).astype(BF16).astype(F32)
         for s in range(4):
-            qkv = lax.dot_general(a_norm, w_ref[s, 0:384, :], NT, preferred_element_type=F32).astype(BF16)
-            q_wide, k_wide = qkv[:, 0:128].astype(F32), qkv[:, 128:256].astype(F32)
-            q_scr[s, rows, :] = (q_wide * cos_tab + pltpu.roll(q_wide, 64, 1) * sin_tab).astype(BF16)
-            k_scr[s, rows, :] = (k_wide * cos_tab + pltpu.roll(k_wide, 64, 1) * sin_tab).astype(BF16)
-            v_scr[s, rows, :] = qkv[:, 256:384]
+            k_wide = keys[:, 128 * s:128 * s + 128]
+            k_scr[s, rows, :] = (k_wide * row_ref[0, rows, :] + pltpu.roll(k_wide, 64, 1) * row_ref[1, rows, :]).astype(BF16)
+        w_qv = w_ref[:, 0:256, :].reshape(2 * width, width)
+        qv = lax.dot_general(w_qv, a_norm, NT, preferred_element_type=F32).astype(BF16)
+        cos_tab, sin_tab = lane_ref[0, :, rows], lane_ref[1, :, rows]
+        for s in range(4):
+            first, second = qv[256 * s:256 * s + 64, :].astype(F32), qv[256 * s + 64:256 * s + 128, :].astype(F32)
+            q_scr[s, 0:64, rows] = (first * cos_tab - second * sin_tab).astype(BF16)
+            q_scr[s, 64:128, rows] = (second * cos_tab + first * sin_tab).astype(BF16)
+            v_scr[s, :, rows] = qv[256 * s + 128:256 * s + 256, :]
         return carry
 
     lax.fori_loop(0, 2, norm_rows, 0)
 
     def head_pair(s, carry):
-        row = lax.broadcasted_iota(jnp.int32, (half, half), 0)
-        col = lax.broadcasted_iota(jnp.int32, (half, half), 1)
-        causal = row >= col
-        outs = [None, None]
+        causal = lax.broadcasted_iota(jnp.int32, (half, half), 0) <= lax.broadcasted_iota(jnp.int32, (half, half), 1)
+        row = lax.broadcasted_iota(jnp.int32, (128, 1), 0)
         for hh in range(2):
-            q_mask = jnp.where((lane // 32) % 2 == hh, 0.125, 0.0).astype(BF16)
-            v_mask = jnp.where(lane // 64 == hh, 1.0, 0.0).astype(BF16)
-            keys = [k_scr[s, 0:half, :], k_scr[s, half:seq, :]]
-            vals = [v_scr[s, 0:half, :] * v_mask, v_scr[s, half:seq, :] * v_mask]
+            q_mask = jnp.where((row // 32) % 2 == hh, 0.125, 0.0).astype(BF16)
             for qb in range(2):
-                q_blk = q_scr[s, qb * half:(qb + 1) * half, :] * q_mask
-                scores = [lax.dot_general(q_blk, keys[kb], NT, preferred_element_type=F32) for kb in range(qb + 1)]
+                cols = slice(qb * half, (qb + 1) * half)
+                q_blk = q_scr[s, :, cols] * q_mask
+                scores = [jnp.dot(k_scr[s, kb * half:(kb + 1) * half, :], q_blk, preferred_element_type=F32) for kb in range(qb + 1)]
                 scores[qb] = jnp.where(causal, scores[qb], -1e30)
-                peak = functools.reduce(jnp.maximum, [jnp.max(sc, axis=-1, keepdims=True) for sc in scores])
+                peak = functools.reduce(jnp.maximum, [jnp.max(sc, axis=0, keepdims=True) for sc in scores])
                 exps = [jnp.exp(sc - peak) for sc in scores]
-                total = functools.reduce(jnp.add, [jnp.sum(e, axis=-1, keepdims=True) for e in exps])
+                total = functools.reduce(jnp.add, [jnp.sum(e, axis=0, keepdims=True) for e in exps])
                 inv = 1.0 / total
-                for kb in range(qb + 1):
-                    part = jnp.dot((exps[kb] * inv).astype(BF16), vals[kb], preferred_element_type=F32)
-                    outs[qb] = part if outs[qb] is None else outs[qb] + part
-        for qb in range(2):
-            o_scr[qb * half:(qb + 1) * half, pl.ds(pl.multiple_of(s * 128, 128), 128)] = outs[qb].astype(BF16)
+                probs = jnp.concatenate([(e * inv).astype(BF16) for e in exps], 0)
+                head_out = jnp.dot(v_scr[s, 64 * hh:64 * hh + 64, 0:(qb + 1) * half], probs, preferred_element_type=F32)
+                o_scr[pl.ds(pl.multiple_of(s * 128 + 64 * hh, 64), 64), cols] = head_out.astype(BF16)
         return carry
 
     lax.fori_loop(0, 4, head_pair, 0)
@@ -85,17 +86,16 @@
     def out_rows(r, carry):
         rows = pl.ds(pl.multiple_of(r * half, half), half)
         w_out = w_ref[:, 384:512, :].reshape(width, width)
-        acc_scr[rows, :] = x_ref[rows, :].astype(F32) + jnp.dot(o_scr[rows, :], w_out, preferred_element_type=F32)
+        heads = lax.dot_general(o_scr[:, rows], w_out, (((0,), (0,)), ((), ())), preferred_element_type=F32)
+        acc_scr[rows, :] = x_ref[rows, :].astype(F32) + heads
         return carry
 
     lax.fori_loop(0, 2, out_rows, 0)
 
     def mlp_part(c, carry):
-        for r in range(2):
-            rows = slice(r * half, (r + 1) * half)
-            pre = jnp.dot(m_scr[rows, :], w_ref[c, 512:1024, :], preferred_element_type=F32)
-            hidden = (0.5 * pre * (1.0 + lax.erf(pre * 0.7071067811865476))).astype(BF16)
-            acc_scr[rows, :] += jnp.dot(hidden, w_ref[c, 1024:1536, :], preferred_element_type=F32)
+        pre = jnp.dot(m_scr[...], w_ref[c, 512:1024, :], preferred_element_type=F32)
+        hidden = (0.5 * pre * (1.0 + lax.erf(pre * 0.7071067811865476))).astype(BF16)
+        acc_scr[...] += jnp.dot(hidden, w_ref[c, 1024:1536, :], preferred_element_type=F32)
         return carry
 
     lax.fori_loop(0, 4, mlp_part, 0)
@@ -199,8 +199,9 @@
         if hop == 0:
             for i in range(8):
                 x_local(i).start()
-        send_x(2 * hop)
-        send_x(2 * hop + 1)
+        if hop == 3:
+            for i in range(8):
+                send_x(i)
 
     @pl.when(p == 0)
     def _():
@@ -325,9 +326,9 @@
                 pltpu.VMEM((2, batch // 4, seq, width), BF16),
                 pltpu.VMEM((rows, width), BF16),
                 pltpu.VMEM((seq, width), BF16),
+                pltpu.VMEM((4, 128, seq), BF16),
                 pltpu.VMEM((4, seq, 128), BF16),
-                pltpu.VMEM((4, seq, 128), BF16),
-                pltpu.VMEM((4, seq, 128), BF16),
+                pltpu.VMEM((4, 128, seq), BF16),
                 pltpu.VMEM((seq, width), BF16),
                 pltpu.VMEM((seq, width), F32),
                 dma((2, 8)), dma, dma, dma((8, 3)), dma, dma((8, 3)), dma((8,)),

time: 349 us -> 292 us (0.84); the launches traced: 345 us -> 292 us
  Pallas kernels: 329 us -> 274 us
    pallas_call x1, Pallas kernels: 329 us -> 274 us  [body(): pl.pallas_call(kernel, out_shape=(emit_shape, emit_shape, jax.ShapeDtypeS...]
where the time goes in v2:
time: 292 us
  Pallas kernels  274 us (94%)
  local copies, waits for them, and re-layouts  11.5 us (4%)
  other arithmetic  5.34 us (2%)
    pallas_call x1, Pallas kernels, body(): pl.pallas_call(kernel, out_shape=(emit_shape, emit_shape, jax.ShapeDtypeS...  274 us
    unnamed x20, local copies, waits for them, and re-layouts  9.57 us

profile of v2, /device:TPU:1, one launch (start us, length us, event | category | flops | bytes accessed | tf_op | source)
XLA Modules:
  0.0 292.1 jit_solution(18005711394621841856)
XLA Ops:
  0.6 0.7 convert_element_type.12
  1.3 1.3 pad_maximum_fusion.2.ln_ref
  2.6 0.9 slice.13
  3.6 0.3 multiply_cosine_fusion.1
  3.9 0.7 pad_maximum_fusion.1.sin_ref
  4.6 1.0 fusion.1
  5.6 1.0 multiply_cosine_fusion
  6.6 0.0 copy-start.3
  6.7 0.0 copy-start.1
  6.7 0.5 maximum_bitcast_fusion
  7.1 0.0 copy-start.2
  7.2 0.8 pad_maximum_fusion.cos_ref
  8.0 0.0 copy-done.3
  8.1 0.0 copy-done.1
  8.1 0.3 copy-done.2
  8.5 0.0 copy-start.4
  8.5 1.1 copy-done.4
  9.6 274.4 %shard_map.112 = (bf16[32,128,128]{2,1,0:T(8,128)(2,1)}, bf16[32,128,128]{2,1,0:T(8,128)(2,1)}, bf16[1,32,128,512]{3,2,1,0:T(8,128)(2,1)}) custom-call(bf16[1,32,128,512]{3,2,1,0:T(8,128)(2,1)} %buf_ref.1, bf16[32,128,512]{2,1,0:T(8,128)(2,1)} %mb_ref.1, bf16[1536,512]{1,0:T(8,128)(2,1)} %copy-done.4, f32[4,512]{1,0:T(4,128)} %pad_maximum_fusion.2.ln_ref, ...), custom_call_target="tpu_custom_call" | custom-call | flops 60000002048 | bytes 40000000 | tf_op jit(solution)/shard_map/pallas_call | solution.py:319
  284.1 0.0 copy-start
  284.1 2.4 copy.27
  286.5 0.0 copy-done
  286.5 1.0 copy.28
  287.4 4.6 %copy.29 = bf16[1,32,128,512]{3,2,1,0:T(8,128)(2,1)} copy(bf16[1,32,128,512]{3,2,1,0:T(8,128)(2,1)} %get-tuple-element.19) | data formatting | bytes 8388608
  (10 shorter events, 0.2 us)
Async XLA Ops:
  6.6 1.4 copy-start.3
  6.7 1.4 copy-start.1
  7.1 1.3 copy-start.2
  8.5 1.1 copy-start.4
  284.1 2.4 copy-start

commit v3 on v2

--- a/solution.py
+++ b/solution.py
@@ -2,6 +2,7 @@
 
 import jax
 import jax.numpy as jnp
+import numpy as np
 from jax import lax
 from jax.experimental import pallas as pl
 from jax.experimental.pallas import tpu as pltpu
@@ -15,22 +16,12 @@
 BF16 = jnp.bfloat16
 
 
-def rope_tables(positions, head_dim):
-    inv_freq = 1.0 / (ROPE_BASE ** (jnp.arange(0, head_dim, 2).astype(F32) / head_dim))
-    angles = positions.astype(F32)[:, None] * inv_freq[None, :]
-    cos_tab, sin_tab = jnp.cos(angles), jnp.sin(angles)
-    by_row = jnp.stack([jnp.concatenate([cos_tab] * 4, 1), jnp.concatenate([-sin_tab, -sin_tab, sin_tab, sin_tab], 1)])
-    by_lane = jnp.stack([jnp.concatenate([cos_tab.T] * 2, 0), jnp.concatenate([sin_tab.T] * 2, 0)])
-    return by_row, by_lane
-
-
-def pack_weights(w_qkv, w_out, w_up, w_down):
-    heads, three, head_dim, width = w_qkv.shape
-    halves = w_qkv.reshape(heads, three, 2, head_dim // 2, width)
-    queries = halves[:, 0].transpose(1, 0, 2, 3).reshape(-1, width)
-    keys = halves[:, 1].transpose(1, 0, 2, 3).reshape(-1, width)
-    values = w_qkv[:, 2].reshape(-1, width)
-    return jnp.concatenate([queries, values, keys, w_out, w_up, w_down], 0)
+def rope_angles(positions, inv_freq):
+    seq = positions.shape[1]
+    by_row = jnp.broadcast_to(positions.astype(F32), (128, seq)).T * inv_freq
+    sign = jnp.where(lax.broadcasted_iota(jnp.int32, (1, 128), 1) < 64, -1.0, 1.0)
+    cos_tab, sin_tab = jnp.cos(by_row), jnp.sin(by_row)
+    return cos_tab, sin_tab * sign, cos_tab.T[64:128, :], sin_tab.T[64:128, :]
 
 
 def layer(x_ref, w_ref, ln_ref, row_ref, lane_ref, m_scr, q_scr, k_scr, v_scr, o_scr, acc_scr):
@@ -40,11 +31,12 @@
     def norm_rows(r, carry):
         rows = pl.ds(pl.multiple_of(r * half, half), half)
         x_wide = x_ref[rows, :].astype(F32)
+        acc_scr[rows, :] = x_wide
         centered = x_wide - jnp.mean(x_wide, axis=-1, keepdims=True)
         variance = jnp.mean(centered * centered, axis=-1, keepdims=True)
         normed = centered * lax.rsqrt(variance + LN_EPS)
-        a_norm = (normed * ln_ref[0:1, :] + ln_ref[1:2, :]).astype(BF16)
-        m_scr[rows, :] = (normed * ln_ref[2:3, :] + ln_ref[3:4, :]).astype(BF16)
+        a_norm = (normed * ln_ref[0, 0:1, :] + ln_ref[0, 1:2, :]).astype(BF16)
+        m_scr[rows, :] = (normed * ln_ref[1, 0:1, :] + ln_ref[1, 1:2, :]).astype(BF16)
         w_k = w_ref[:, 256:384, :].reshape(width, width)
         keys = lax.dot_general(a_norm, w_k, NT, preferred_element_type=F32).astype(BF16).astype(F32)
         for s in range(4):
@@ -60,9 +52,10 @@
             v_scr[s, :, rows] = qv[256 * s + 128:256 * s + 256, :]
         return carry
 
-    lax.fori_loop(0, 2, norm_rows, 0)
-
-    def head_pair(s, carry):
+    lax.fori_loop(0, 2, norm_rows, 0, unroll=2)
+
+    def head_pair_and_mlp_part(s, carry):
+        pre = jnp.dot(m_scr[...], w_ref[s, 512:1024, :], preferred_element_type=F32)
         causal = lax.broadcasted_iota(jnp.int32, (half, half), 0) <= lax.broadcasted_iota(jnp.int32, (half, half), 1)
         row = lax.broadcasted_iota(jnp.int32, (128, 1), 0)
         for hh in range(2):
@@ -75,37 +68,29 @@
                 peak = functools.reduce(jnp.maximum, [jnp.max(sc, axis=0, keepdims=True) for sc in scores])
                 exps = [jnp.exp(sc - peak) for sc in scores]
                 total = functools.reduce(jnp.add, [jnp.sum(e, axis=0, keepdims=True) for e in exps])
-                inv = 1.0 / total
-                probs = jnp.concatenate([(e * inv).astype(BF16) for e in exps], 0)
+                probs = jnp.concatenate([e.astype(BF16) for e in exps], 0)
                 head_out = jnp.dot(v_scr[s, 64 * hh:64 * hh + 64, 0:(qb + 1) * half], probs, preferred_element_type=F32)
-                o_scr[pl.ds(pl.multiple_of(s * 128 + 64 * hh, 64), 64), cols] = head_out.astype(BF16)
+                o_scr[pl.ds(pl.multiple_of(s * 128 + 64 * hh, 64), 64), cols] = (head_out * (1.0 / total)).astype(BF16)
+        hidden = (0.5 * pre * (1.0 + lax.erf(pre * 0.7071067811865476))).astype(BF16)
+        acc_scr[...] += jnp.dot(hidden, w_ref[s, 1024:1536, :], preferred_element_type=F32)
         return carry
 
-    lax.fori_loop(0, 4, head_pair, 0)
+    lax.fori_loop(0, 4, head_pair_and_mlp_part, 0, unroll=4)
 
     def out_rows(r, carry):
         rows = pl.ds(pl.multiple_of(r * half, half), half)
         w_out = w_ref[:, 384:512, :].reshape(width, width)
         heads = lax.dot_general(o_scr[:, rows], w_out, (((0,), (0,)), ((), ())), preferred_element_type=F32)
-        acc_scr[rows, :] = x_ref[rows, :].astype(F32) + heads
+        x_ref[rows, :] = (acc_scr[rows, :] + heads).astype(BF16)
         return carry
 
-    lax.fori_loop(0, 2, out_rows, 0)
-
-    def mlp_part(c, carry):
-        pre = jnp.dot(m_scr[...], w_ref[c, 512:1024, :], preferred_element_type=F32)
-        hidden = (0.5 * pre * (1.0 + lax.erf(pre * 0.7071067811865476))).astype(BF16)
-        acc_scr[...] += jnp.dot(hidden, w_ref[c, 1024:1536, :], preferred_element_type=F32)
-        return carry
-
-    lax.fori_loop(0, 4, mlp_part, 0)
-    x_ref[...] = acc_scr[...].astype(BF16)
-
-
-def kernel(buf_ref, mb_ref, w_loc, ln_ref, cos_ref, sin_ref, emit_one, emit_two, final,
-           w_all, xs, zeros, m_scr, q_scr, k_scr, v_scr, o_scr, acc_scr,
-           loc_sem, wloc_sem, xs_send, xs_recv, mb_send, mb_recv, y_recv, wz_send, wz_recv, wx_send, wx_recv,
-           y_send, emit_recv, final_recv, zero_sem):
+    lax.fori_loop(0, 2, out_rows, 0, unroll=2)
+
+
+def kernel(buf_ref, mb_ref, pos_ref, freq_ref, ln_attn, ln_mlp, w_qkv, w_out, w_up, w_down, emit_one, emit_two, final,
+           w_all, xs, ln_scr, row_scr, lane_scr, m_scr, q_scr, k_scr, v_scr, o_scr, acc_scr,
+           loc_sem, wloc_sem, ln_sem, xs_send, xs_recv, mb_send, mb_recv, y_recv, wz_send, wz_recv, wx_send, wx_recv,
+           y_send, emit_recv, final_recv):
     d, t, p = lax.axis_index("dp"), lax.axis_index("tp"), lax.axis_index("pp")
     emits = (emit_one, emit_two)
 
@@ -149,10 +134,9 @@
         size = 256 * (piece + 1)
         return pl.ds(pl.multiple_of(512 * piece + dp * size, 256), size)
 
-    def w_copy_z(s, piece, to, slot, own):
+    def w_copy_z(s, piece, to, slot):
         rows = half_rows(d, piece)
-        src = w_loc.at[rows, :] if own else w_all.at[s, rows, :]
-        return remote(src, w_all.at[s, rows, :], wz_send.at[slot, piece], wz_recv.at[s, piece], tp=to)
+        return remote(w_all.at[s, rows, :], w_all.at[s, rows, :], wz_send.at[slot, piece], wz_recv.at[s, piece], tp=to)
 
     def w_copy_x(s, piece):
         rows = half_rows(d, piece)
@@ -171,11 +155,11 @@
                 if hop < 3:
                     @pl.when(jnp.logical_and(from_left, t < 3))
                     def _():
-                        action("z", w_copy_z(right_src, piece, lax.min(t + 1, 3), 2 * hop, hop == 0), right_src, piece)
+                        action("z", w_copy_z(right_src, piece, lax.min(t + 1, 3), 2 * hop), right_src, piece)
 
                     @pl.when(jnp.logical_and(from_right, t > 0))
                     def _():
-                        action("z", w_copy_z(left_src, piece, lax.max(t - 1, 0), 2 * hop + 1, hop == 0), left_src, piece)
+                        action("z", w_copy_z(left_src, piece, lax.max(t - 1, 0), 2 * hop + 1), left_src, piece)
                 if hop:
                     for arrived, s in ((from_left, right_src), (from_right, left_src)):
                         @pl.when(arrived)
@@ -193,15 +177,26 @@
         if kind != "arrive":
             copy.wait_send()
 
-    own_w = pltpu.make_async_copy(w_loc, w_all.at[t], wloc_sem)
-    own_w.start()
+    own = []
+    for head in range(2):
+        for j, row in ((0, 0), (1, 256)):
+            for side in range(2):
+                own.append((w_qkv.at[0, head, j, pl.ds(32 * side, 32), :], row + 64 * side + 32 * head, 32))
+        own.append((w_qkv.at[0, head, 2], 128 + 64 * head, 64))
+    own += [(w_out.at[0], 384, 128), (w_up.at[0], 512, 512), (w_down.at[0], 1024, 512)]
+    for src, row, size in own:
+        pltpu.make_async_copy(src, w_all.at[t, pl.ds(row, size), :], wloc_sem).start()
+    small = [pltpu.make_async_copy(ln_attn.at[0], ln_scr.at[0], ln_sem.at[0]), pltpu.make_async_copy(ln_mlp.at[0], ln_scr.at[1], ln_sem.at[1])]
+    for copy in small:
+        copy.start()
+    send_x(0)
+    wait_bytes(w_all.at[t], wloc_sem)
     for hop in relay(start_or_wait):
         if hop == 0:
             for i in range(8):
                 x_local(i).start()
-        if hop == 3:
-            for i in range(8):
-                send_x(i)
+        for i in ((), (1, 2), (3, 4), (5, 6, 7))[hop]:
+            send_x(i)
 
     @pl.when(p == 0)
     def _():
@@ -211,14 +206,15 @@
                 mb_copy(i, o).start()
             return carry
         lax.fori_loop(0, 8, body, 0)
-        zeros[...] = jnp.zeros_like(zeros)
 
         def zero_body(i, carry):
-            pltpu.make_async_copy(zeros, final.at[0, i], zero_sem).start()
+            final[0, i] = jnp.zeros(final.shape[2:], BF16)
             return carry
         lax.fori_loop(0, 32, zero_body, 0)
 
-    own_w.wait()
+    for copy in small:
+        copy.wait()
+    row_scr[0], row_scr[1], lane_scr[0], lane_scr[1] = rope_angles(pos_ref[...], freq_ref[...])
     for o in (1, 2, 3):
         src = lax.rem(t + 4 - o, 4)
         for piece in range(2):
@@ -229,8 +225,6 @@
         q = lax.rem(3 + qq, 4)
         src = xs.at[tick, i, seq_rows(to), seq_rows(q)]
         dst = emits[tick].at[8 * t + i]
-        if o == 0 and qq == 0:
-            return pltpu.make_async_copy(src, dst, emit_recv.at[tick, 0])
         return remote(src, dst, y_send.at[tick, i], emit_recv.at[tick, o], tp=to, pp=q)
 
     def tick_body(tick):
@@ -249,7 +243,7 @@
                 @pl.when(p > 0)
                 def _():
                     wait_bytes(xs.at[1, i], y_recv.at[i])
-            layer(xs.at[tick, i], w_all, ln_ref, cos_ref, sin_ref, m_scr, q_scr, k_scr, v_scr, o_scr, acc_scr)
+            layer(xs.at[tick, i], w_all, ln_scr, row_scr, lane_scr, m_scr, q_scr, k_scr, v_scr, o_scr, acc_scr)
 
             @pl.when(p < 3)
             def _():
@@ -266,7 +260,10 @@
             def _():
                 for o in (2, 1, 3, 0):
                     for qq in (1, 2, 3, 0):
-                        emit_copy(tick, i, o, qq).start()
+                        if o == 0 and qq == 0:
+                            emits[tick][8 * t + i] = xs[tick, i, seq_rows(t), 384:512]
+                        else:
+                            emit_copy(tick, i, o, qq).start()
             return carry
         lax.fori_loop(0, 8, step, 0)
 
@@ -280,7 +277,6 @@
     @pl.when(p == 0)
     def _():
         wait_bytes(mb_ref.at[0:24], mb_send)
-        wait_bytes(final.at[0], zero_sem)
 
     @pl.when(p > 0)
     def _():
@@ -290,8 +286,9 @@
 
     for tick in range(2):
         for o in range(4):
-            src = lax.rem(t + 4 - o, 4)
-            wait_bytes(emits[tick].at[pl.ds(8 * src, 8)], emit_recv.at[tick, o])
+            @pl.when(jnp.logical_or(p < 3, o > 0))
+            def _():
+                wait_bytes(emits[tick].at[pl.ds(8 * lax.rem(t + 4 - o, 4), 8)], emit_recv.at[tick, o])
 
         def sent(i, carry):
             @pl.when(p < 3)
@@ -307,37 +304,40 @@
 
 def solution(mesh):
     def body(stage_buf, new_mb, positions, ln_attn, ln_mlp, w_qkv, w_out, w_up, w_down):
-        cos_tab, sin_tab = rope_tables(positions, w_qkv.shape[3])
-        packed = pack_weights(w_qkv[0], w_out[0], w_up[0], w_down[0])
-        ln_rows = jnp.concatenate([ln_attn[0], ln_mlp[0]], 0)
+        head_dim = w_qkv.shape[3]
+        inv_freq = 1.0 / np.power(np.float32(ROPE_BASE), np.arange(0, head_dim, 2).astype(np.float32) / np.float32(head_dim))
+        inv_freq = jnp.asarray(np.tile(inv_freq.astype(np.float32), 4)[None])
         batch, rows, width = new_mb.shape
         seq = 4 * rows
         emit_shape = jax.ShapeDtypeStruct((batch, rows, width // 4), BF16)
         hbm = pl.BlockSpec(memory_space=pl.ANY)
         vmem = pl.BlockSpec(memory_space=pltpu.VMEM)
         dma = pltpu.SemaphoreType.DMA
+        shapes = (emit_shape, emit_shape, jax.ShapeDtypeStruct(stage_buf.shape, BF16))
         return pl.pallas_call(
             kernel,
-            out_shape=(emit_shape, emit_shape, jax.ShapeDtypeStruct(stage_buf.shape, BF16)),
-            in_specs=[hbm, hbm, hbm, vmem, vmem, vmem],
-            out_specs=(hbm, hbm, hbm),
+            out_shape=tuple(pltpu.VMEM(sh.shape, BF16) for sh in shapes),
+            in_specs=[hbm, hbm, vmem, vmem, hbm, hbm, hbm, hbm, hbm, hbm],
+            out_specs=(vmem, vmem, vmem),
             scratch_shapes=[
                 pltpu.VMEM((4, 1536, width), BF16),
                 pltpu.VMEM((2, batch // 4, seq, width), BF16),
-                pltpu.VMEM((rows, width), BF16),
+                pltpu.VMEM((2, 2, width), F32),
+                pltpu.VMEM((2, seq, 128), F32),
+                pltpu.VMEM((2, 64, seq), F32),
                 pltpu.VMEM((seq, width), BF16),
                 pltpu.VMEM((4, 128, seq), BF16),
                 pltpu.VMEM((4, seq, 128), BF16),
                 pltpu.VMEM((4, 128, seq), BF16),
                 pltpu.VMEM((seq, width), BF16),
                 pltpu.VMEM((seq, width), F32),
-                dma((2, 8)), dma, dma, dma((8, 3)), dma, dma((8, 3)), dma((8,)),
+                dma((2, 8)), dma, dma((2,)), dma, dma((8, 3)), dma, dma((8, 3)), dma((8,)),
                 dma((6, 2)), dma((4, 2)), dma((4, 2)), dma((4, 2)),
-                dma((2, 8)), dma((2, 4)), dma((4,)), dma,
+                dma((2, 8)), dma((2, 4)), dma((4,)),
             ],
-            compiler_params=pltpu.CompilerParams(has_side_effects=True, vmem_limit_bytes=60 * 1024 * 1024),
+            compiler_params=pltpu.CompilerParams(has_side_effects=True, vmem_limit_bytes=57 * 1024 * 1024),
             cost_estimate=pl.CostEstimate(flops=60_000_000_000, bytes_accessed=40_000_000, transcendentals=50_000_000),
-        )(stage_buf, new_mb, packed, ln_rows, cos_tab, sin_tab)
+        )(stage_buf, new_mb, positions[None, :], inv_freq, ln_attn, ln_mlp, w_qkv, w_out, w_up, w_down)
 
     act_spec = P("dp", "tp", None)
     buf_spec = P("pp", "dp", "tp", None)

time: 292 us -> 276 us (0.945)
  local copies, waits for them, and re-layouts: 11.5 us -> 3.95 us
  other arithmetic: 5.34 us -> 0 us
  Pallas kernels: 274 us -> 271 us
    unnamed x20 -> x3, local copies, waits for them, and re-layouts: 9.57 us -> 3.95 us
    pallas_call x1, Pallas kernels: 274 us -> 271 us  [body(): pl.pallas_call(kernel, out_shape=tuple((pltpu.VMEM(sh.shape, BF16) for sh...]
where the time goes in v3:
time: 276 us
  Pallas kernels  271 us (98%)
  local copies, waits for them, and re-layouts  3.95 us (1%)
    pallas_call x1, Pallas kernels, body(): pl.pallas_call(kernel, out_shape=tuple((pltpu.VMEM(sh.shape, BF16) for sh...  271 us

profile of v3, /device:TPU:1, one launch (start us, length us, event | category | flops | bytes accessed | tf_op | source)
XLA Modules:
  0.0 276.1 jit_solution(7434931424726993518)
XLA Ops:
  0.6 271.5 %shard_map.121 = (bf16[32,128,128]{2,1,0:T(8,128)(2,1)S(1)}, bf16[32,128,128]{2,1,0:T(8,128)(2,1)S(1)}, bf16[1,32,128,512]{3,2,1,0:T(8,128)(2,1)S(1)}) custom-call(bf16[1,32,128,512]{3,2,1,0:T(8,128)(2,1)} %buf_ref.1, bf16[32,128,512]{2,1,0:T(8,128)(2,1)} %mb_ref.1, s32[1,512]{1,0:T(1,128)} %bitcast.1, f32[1,128]{1,0:T(1,128)} %constant.2.clone.freq_ref, ...), custom_call_target="tpu_custom_call" | custom-call | flops 60000002048 | bytes 40000000 | tf_op jit(solution)/shard_map/pallas_call | solution.py:317
  272.1 1.0 copy.16
  273.1 1.0 copy.17
  274.1 2.0 copy.18

commit v4 on v3

--- a/solution.py
+++ b/solution.py
@@ -189,12 +189,21 @@
     small = [pltpu.make_async_copy(ln_attn.at[0], ln_scr.at[0], ln_sem.at[0]), pltpu.make_async_copy(ln_mlp.at[0], ln_scr.at[1], ln_sem.at[1])]
     for copy in small:
         copy.start()
+    for i in range(8):
+        x_local(i).start()
+
+    barrier = pltpu.get_barrier_semaphore()
+    for o in range(4):
+        for oo in range(4):
+            if o or oo:
+                where = (d, lax.rem(t + o, 4), lax.rem(p + oo, 4))
+                pl.semaphore_signal(barrier, inc=1, device_id=where, device_id_type=MESH)
+    pl.semaphore_signal(barrier, inc=1, device_id=(1 - d, t, p), device_id_type=MESH)
+    pl.semaphore_wait(barrier, 16)
+
     send_x(0)
     wait_bytes(w_all.at[t], wloc_sem)
     for hop in relay(start_or_wait):
-        if hop == 0:
-            for i in range(8):
-                x_local(i).start()
         for i in ((), (1, 2), (3, 4), (5, 6, 7))[hop]:
             send_x(i)
 
@@ -335,7 +344,7 @@
                 dma((6, 2)), dma((4, 2)), dma((4, 2)), dma((4, 2)),
                 dma((2, 8)), dma((2, 4)), dma((4,)),
             ],
-            compiler_params=pltpu.CompilerParams(has_side_effects=True, vmem_limit_bytes=57 * 1024 * 1024),
+            compiler_params=pltpu.CompilerParams(has_side_effects=True, collective_id=0, vmem_limit_bytes=57 * 1024 * 1024),
             cost_estimate=pl.CostEstimate(flops=60_000_000_000, bytes_accessed=40_000_000, transcendentals=50_000_000),
         )(stage_buf, new_mb, positions[None, :], inv_freq, ln_attn, ln_mlp, w_qkv, w_out, w_up, w_down)
 

time: 276 us -> 273 us (0.989)
    pallas_call x1, Pallas kernels: 271 us -> 269 us  [body(): pl.pallas_call(kernel, out_shape=tuple((pltpu.VMEM(sh.shape, BF16) for sh...]
where the time goes in v4:
time: 273 us
  Pallas kernels  269 us (99%)
  local copies, waits for them, and re-layouts  3.95 us (1%)
    pallas_call x1, Pallas kernels, body(): pl.pallas_call(kernel, out_shape=tuple((pltpu.VMEM(sh.shape, BF16) for sh...  269 us

profile of v4, /device:TPU:1, one launch (start us, length us, event | category | flops | bytes accessed | tf_op | source)
XLA Modules:
  0.0 273.2 jit_solution(12490627763373606948)
XLA Ops:
  0.6 268.6 %shard_map.121 = (bf16[32,128,128]{2,1,0:T(8,128)(2,1)S(1)}, bf16[32,128,128]{2,1,0:T(8,128)(2,1)S(1)}, bf16[1,32,128,512]{3,2,1,0:T(8,128)(2,1)S(1)}) custom-call(bf16[1,32,128,512]{3,2,1,0:T(8,128)(2,1)} %buf_ref.1, bf16[32,128,512]{2,1,0:T(8,128)(2,1)} %mb_ref.1, s32[1,512]{1,0:T(1,128)} %bitcast.1, f32[1,128]{1,0:T(1,128)} %constant.2.clone.freq_ref, ...), custom_call_target="tpu_custom_call" | custom-call | flops 60000002048 | bytes 40000000 | tf_op jit(solution)/shard_map/pallas_call | solution.py:326
  269.3 1.0 copy.16
  270.2 1.0 copy.17
  271.2 2.0 copy.18

commit v5 on v4

--- a/solution.py
+++ b/solution.py
@@ -88,7 +88,7 @@
 
 
 def kernel(buf_ref, mb_ref, pos_ref, freq_ref, ln_attn, ln_mlp, w_qkv, w_out, w_up, w_down, emit_one, emit_two, final,
-           w_all, xs, ln_scr, row_scr, lane_scr, m_scr, q_scr, k_scr, v_scr, o_scr, acc_scr,
+           w_all, xs, pos_scr, freq_scr, ln_scr, row_scr, lane_scr, m_scr, q_scr, k_scr, v_scr, o_scr, acc_scr,
            loc_sem, wloc_sem, ln_sem, xs_send, xs_recv, mb_send, mb_recv, y_recv, wz_send, wz_recv, wx_send, wx_recv,
            y_send, emit_recv, final_recv):
     d, t, p = lax.axis_index("dp"), lax.axis_index("tp"), lax.axis_index("pp")
@@ -177,6 +177,14 @@
         if kind != "arrive":
             copy.wait_send()
 
+    barrier = pltpu.get_barrier_semaphore()
+    for o in range(4):
+        for oo in range(4):
+            if o or oo:
+                where = (d, lax.rem(t + o, 4), lax.rem(p + oo, 4))
+                pl.semaphore_signal(barrier, inc=1, device_id=where, device_id_type=MESH)
+    pl.semaphore_signal(barrier, inc=1, device_id=(1 - d, t, p), device_id_type=MESH)
+
     own = []
     for head in range(2):
         for j, row in ((0, 0), (1, 256)):
@@ -186,19 +194,13 @@
     own += [(w_out.at[0], 384, 128), (w_up.at[0], 512, 512), (w_down.at[0], 1024, 512)]
     for src, row, size in own:
         pltpu.make_async_copy(src, w_all.at[t, pl.ds(row, size), :], wloc_sem).start()
-    small = [pltpu.make_async_copy(ln_attn.at[0], ln_scr.at[0], ln_sem.at[0]), pltpu.make_async_copy(ln_mlp.at[0], ln_scr.at[1], ln_sem.at[1])]
+    small = [pltpu.make_async_copy(ln_attn.at[0], ln_scr.at[0], ln_sem.at[0]), pltpu.make_async_copy(ln_mlp.at[0], ln_scr.at[1], ln_sem.at[1]),
+             pltpu.make_async_copy(pos_ref, pos_scr, ln_sem.at[2]), pltpu.make_async_copy(freq_ref, freq_scr, ln_sem.at[3])]
     for copy in small:
         copy.start()
     for i in range(8):
         x_local(i).start()
 
-    barrier = pltpu.get_barrier_semaphore()
-    for o in range(4):
-        for oo in range(4):
-            if o or oo:
-                where = (d, lax.rem(t + o, 4), lax.rem(p + oo, 4))
-                pl.semaphore_signal(barrier, inc=1, device_id=where, device_id_type=MESH)
-    pl.semaphore_signal(barrier, inc=1, device_id=(1 - d, t, p), device_id_type=MESH)
     pl.semaphore_wait(barrier, 16)
 
     send_x(0)
@@ -223,7 +225,7 @@
 
     for copy in small:
         copy.wait()
-    row_scr[0], row_scr[1], lane_scr[0], lane_scr[1] = rope_angles(pos_ref[...], freq_ref[...])
+    row_scr[0], row_scr[1], lane_scr[0], lane_scr[1] = rope_angles(pos_scr[...], freq_scr[...])
     for o in (1, 2, 3):
         src = lax.rem(t + 4 - o, 4)
         for piece in range(2):
@@ -311,6 +313,19 @@
         lax.fori_loop(0, 8, sent, 0)
 
 
+def unload(*refs):
+    copies = []
+    for j in range(3):
+        source, target = (refs[j].at[0], refs[3 + j].at[0]) if j == 2 else (refs[j], refs[3 + j])
+        step = source.shape[0] // (4 if j == 2 else 1)
+        for k in range(0, source.shape[0], step):
+            copies.append(pltpu.make_async_copy(source.at[pl.ds(k, step)], target.at[pl.ds(k, step)], refs[6].at[len(copies)]))
+    for copy in copies:
+        copy.start()
+    for copy in copies:
+        copy.wait()
+
+
 def solution(mesh):
     def body(stage_buf, new_mb, positions, ln_attn, ln_mlp, w_qkv, w_out, w_up, w_down):
         head_dim = w_qkv.shape[3]
@@ -323,14 +338,16 @@
         vmem = pl.BlockSpec(memory_space=pltpu.VMEM)
         dma = pltpu.SemaphoreType.DMA
         shapes = (emit_shape, emit_shape, jax.ShapeDtypeStruct(stage_buf.shape, BF16))
-        return pl.pallas_call(
+        landed = pl.pallas_call(
             kernel,
             out_shape=tuple(pltpu.VMEM(sh.shape, BF16) for sh in shapes),
-            in_specs=[hbm, hbm, vmem, vmem, hbm, hbm, hbm, hbm, hbm, hbm],
+            in_specs=[hbm, hbm, hbm, hbm, hbm, hbm, hbm, hbm, hbm, hbm],
             out_specs=(vmem, vmem, vmem),
             scratch_shapes=[
                 pltpu.VMEM((4, 1536, width), BF16),
                 pltpu.VMEM((2, batch // 4, seq, width), BF16),
+                pltpu.VMEM((1, seq), jnp.int32),
+                pltpu.VMEM((1, 128), F32),
                 pltpu.VMEM((2, 2, width), F32),
                 pltpu.VMEM((2, seq, 128), F32),
                 pltpu.VMEM((2, 64, seq), F32),
@@ -340,13 +357,23 @@
                 pltpu.VMEM((4, 128, seq), BF16),
                 pltpu.VMEM((seq, width), BF16),
                 pltpu.VMEM((seq, width), F32),
-                dma((2, 8)), dma, dma((2,)), dma, dma((8, 3)), dma, dma((8, 3)), dma((8,)),
+                dma((2, 8)), dma, dma((4,)), dma, dma((8, 3)), dma, dma((8, 3)), dma((8,)),
                 dma((6, 2)), dma((4, 2)), dma((4, 2)), dma((4, 2)),
                 dma((2, 8)), dma((2, 4)), dma((4,)),
             ],
             compiler_params=pltpu.CompilerParams(has_side_effects=True, collective_id=0, vmem_limit_bytes=57 * 1024 * 1024),
             cost_estimate=pl.CostEstimate(flops=60_000_000_000, bytes_accessed=40_000_000, transcendentals=50_000_000),
         )(stage_buf, new_mb, positions[None, :], inv_freq, ln_attn, ln_mlp, w_qkv, w_out, w_up, w_down)
+        landed = [pltpu.with_memory_space_constraint(x, pltpu.VMEM) for x in landed]
+        return pl.pallas_call(
+            unload,
+            out_shape=shapes,
+            in_specs=[vmem, vmem, vmem],
+            out_specs=(hbm, hbm, hbm),
+            scratch_shapes=[dma((6,))],
+            compiler_params=pltpu.CompilerParams(vmem_limit_bytes=1024 * 1024),
+            cost_estimate=pl.CostEstimate(flops=1_000_000, bytes_accessed=12_000_000, transcendentals=0),
+        )(*landed)
 
     act_spec = P("dp", "tp", None)
     buf_spec = P("pp", "dp", "tp", None)

time: 273 us -> 271 us (level)
  local copies, waits for them, and re-layouts: 3.95 us -> 0 us
    unnamed x3 -> x0, local copies, waits for them, and re-layouts: 3.95 us -> none
where the time goes in v5:
time: 271 us
  Pallas kernels  270 us (100%)
    pallas_call x1, Pallas kernels, body(): pl.pallas_call(kernel, out_shape=tuple((pltpu.VMEM(sh.shape, BF16) for sh...  267 us

profile of v5, /device:TPU:1, one launch (start us, length us, event | category | flops | bytes accessed | tf_op | source)
XLA Modules:
  0.0 270.9 jit_solution(462785152200206498)
XLA Ops:
  0.6 267.4 %shard_map.121 = (bf16[32,128,128]{2,1,0:T(8,128)(2,1)S(1)}, bf16[32,128,128]{2,1,0:T(8,128)(2,1)S(1)}, bf16[1,32,128,512]{3,2,1,0:T(8,128)(2,1)S(1)}) custom-call(bf16[1,32,128,512]{3,2,1,0:T(8,128)(2,1)} %buf_ref.1, bf16[32,128,512]{2,1,0:T(8,128)(2,1)} %mb_ref.1, s32[1,512]{1,0:T(1,128)} %bitcast.1, f32[1,128]{1,0:T(1,128)} %constant.2.clone.freq_ref, ...), custom_call_target="tpu_custom_call" | custom-call | flops 60000002048 | bytes 40000000 | tf_op jit(solution)/shard_map/pallas_call | solution.py:341
  268.1 2.7 %shard_map.122 = (bf16[32,128,128]{2,1,0:T(8,128)(2,1)}, bf16[32,128,128]{2,1,0:T(8,128)(2,1)}, bf16[1,32,128,512]{3,2,1,0:T(8,128)(2,1)}) custom-call(bf16[32,128,128]{2,1,0:T(8,128)(2,1)S(1)} %get-tuple-element.6.refs_0_, bf16[32,128,128]{2,1,0:T(8,128)(2,1)S(1)} %get-tuple-element.7.refs_1_, bf16[1,32,128,512]{3,2,1,0:T(8,128)(2,1)S(1)} %get-tuple-element.8.refs_2_), custom_call_target="tpu_custom_call" | custom-call | flops 1000000 | bytes 12000000 | tf_op jit(solution)/shard_map/pallas_call | solution.py:368

commit v6 on v5

--- a/solution.py
+++ b/solution.py
@@ -90,7 +90,7 @@
 def kernel(buf_ref, mb_ref, pos_ref, freq_ref, ln_attn, ln_mlp, w_qkv, w_out, w_up, w_down, emit_one, emit_two, final,
            w_all, xs, pos_scr, freq_scr, ln_scr, row_scr, lane_scr, m_scr, q_scr, k_scr, v_scr, o_scr, acc_scr,
            loc_sem, wloc_sem, ln_sem, xs_send, xs_recv, mb_send, mb_recv, y_recv, wz_send, wz_recv, wx_send, wx_recv,
-           y_send, emit_recv, final_recv):
+           y_send, emit_recv, final_recv, column_sem):
     d, t, p = lax.axis_index("dp"), lax.axis_index("tp"), lax.axis_index("pp")
     emits = (emit_one, emit_two)
 
@@ -178,11 +178,9 @@
             copy.wait_send()
 
     barrier = pltpu.get_barrier_semaphore()
-    for o in range(4):
-        for oo in range(4):
-            if o or oo:
-                where = (d, lax.rem(t + o, 4), lax.rem(p + oo, 4))
-                pl.semaphore_signal(barrier, inc=1, device_id=where, device_id_type=MESH)
+    for o in (1, 2, 3):
+        pl.semaphore_signal(barrier, inc=1, device_id=(d, lax.rem(t + o, 4), p), device_id_type=MESH)
+        pl.semaphore_signal(barrier, inc=1, device_id=(d, t, lax.rem(p + o, 4)), device_id_type=MESH)
     pl.semaphore_signal(barrier, inc=1, device_id=(1 - d, t, p), device_id_type=MESH)
 
     own = []
@@ -201,9 +199,11 @@
     for i in range(8):
         x_local(i).start()
 
-    pl.semaphore_wait(barrier, 16)
+    pl.semaphore_wait(barrier, 7)
 
     send_x(0)
+    for o in (1, 2, 3):
+        pl.semaphore_signal(column_sem, inc=1, device_id=(d, lax.rem(t + o, 4), p), device_id_type=MESH)
     wait_bytes(w_all.at[t], wloc_sem)
     for hop in relay(start_or_wait):
         for i in ((), (1, 2), (3, 4), (5, 6, 7))[hop]:
@@ -278,6 +278,7 @@
             return carry
         lax.fori_loop(0, 8, step, 0)
 
+    pl.semaphore_wait(column_sem, 3)
     tick_body(0)
     tick_body(1)
 
@@ -359,7 +360,7 @@
                 pltpu.VMEM((seq, width), F32),
                 dma((2, 8)), dma, dma((4,)), dma, dma((8, 3)), dma, dma((8, 3)), dma((8,)),
                 dma((6, 2)), dma((4, 2)), dma((4, 2)), dma((4, 2)),
-                dma((2, 8)), dma((2, 4)), dma((4,)),
+                dma((2, 8)), dma((2, 4)), dma((4,)), pltpu.SemaphoreType.REGULAR,
             ],
             compiler_params=pltpu.CompilerParams(has_side_effects=True, collective_id=0, vmem_limit_bytes=57 * 1024 * 1024),
             cost_estimate=pl.CostEstimate(flops=60_000_000_000, bytes_accessed=40_000_000, transcendentals=50_000_000),

time: 271 us -> 270 us (level)
  no operation moved by 1% of the time
where the time goes in v6:
time: 270 us; the launch traced here: 269 us
  Pallas kernels  268 us (99%)
    pallas_call x1, Pallas kernels, body(): pl.pallas_call(kernel, out_shape=tuple((pltpu.VMEM(sh.shape, BF16) for sh...  266 us

profile of v6, /device:TPU:1, one launch (start us, length us, event | category | flops | bytes accessed | tf_op | source)
XLA Modules:
  0.0 269.1 jit_solution(7449880237326161908)
XLA Ops:
  0.6 265.6 %shard_map.121 = (bf16[32,128,128]{2,1,0:T(8,128)(2,1)S(1)}, bf16[32,128,128]{2,1,0:T(8,128)(2,1)S(1)}, bf16[1,32,128,512]{3,2,1,0:T(8,128)(2,1)S(1)}) custom-call(bf16[1,32,128,512]{3,2,1,0:T(8,128)(2,1)} %buf_ref.1, bf16[32,128,512]{2,1,0:T(8,128)(2,1)} %mb_ref.1, s32[1,512]{1,0:T(1,128)} %bitcast.1, f32[1,128]{1,0:T(1,128)} %constant.2.clone.freq_ref, ...), custom_call_target="tpu_custom_call" | custom-call | flops 60000002048 | bytes 40000000 | tf_op jit(solution)/shard_map/pallas_call | solution.py:342
  266.2 2.7 %shard_map.122 = (bf16[32,128,128]{2,1,0:T(8,128)(2,1)}, bf16[32,128,128]{2,1,0:T(8,128)(2,1)}, bf16[1,32,128,512]{3,2,1,0:T(8,128)(2,1)}) custom-call(bf16[32,128,128]{2,1,0:T(8,128)(2,1)S(1)} %get-tuple-element.6.refs_0_, bf16[32,128,128]{2,1,0:T(8,128)(2,1)S(1)} %get-tuple-element.7.refs_1_, bf16[1,32,128,512]{3,2,1,0:T(8,128)(2,1)S(1)} %get-tuple-element.8.refs_2_), custom_call_target="tpu_custom_call" | custom-call | flops 1000000 | bytes 12000000 | tf_op jit(solution)/shard_map/pallas_call | solution.py:369

commit v7 on v6

--- a/solution.py
+++ b/solution.py
@@ -93,6 +93,8 @@
            y_send, emit_recv, final_recv, column_sem):
     d, t, p = lax.axis_index("dp"), lax.axis_index("tp"), lax.axis_index("pp")
     emits = (emit_one, emit_two)
+    second = 3 - 2 * lax.min(t, 1)
+    outward = (2, second, 4 - second)
 
     def remote(src, dst, send, recv, dp=None, tp=None, pp=None):
         where = (d if dp is None else dp, t if tp is None else tp, p if pp is None else pp)
@@ -127,7 +129,7 @@
         return pltpu.make_async_copy(mb_ref.at[8 * t + i], xs.at[1, i, seq_rows(t), :], loc_sem.at[1, i])
 
     def send_x(i):
-        for o in (2, 1, 3):
+        for o in outward:
             x_copy(i, o).start()
 
     def half_rows(dp, piece):
@@ -213,7 +215,7 @@
     def _():
         def body(i, carry):
             mb_local(i).start()
-            for o in (2, 1, 3):
+            for o in outward:
                 mb_copy(i, o).start()
             return carry
         lax.fori_loop(0, 8, body, 0)
@@ -262,16 +264,16 @@
                 if tick == 0:
                     remote(xs.at[0, i], xs.at[1, i], y_send.at[0, i], y_recv.at[i], pp=nxt).start()
                 else:
-                    for o in (2, 1, 3, 0):
+                    for o in outward + (0,):
                         to = lax.rem(t + o, 4)
                         remote(xs.at[1, i, seq_rows(to), :], final.at[0, 8 * t + i], y_send.at[1, i], final_recv.at[o],
                                tp=to, pp=nxt).start()
 
             @pl.when(p == 3)
             def _():
-                for o in (2, 1, 3, 0):
+                for o in outward + (0,):
                     for qq in (1, 2, 3, 0):
-                        if o == 0 and qq == 0:
+                        if isinstance(o, int) and o == 0 and qq == 0:
                             emits[tick][8 * t + i] = xs[tick, i, seq_rows(t), 384:512]
                         else:
                             emit_copy(tick, i, o, qq).start()

time: 270 us -> 270 us (level)
  no operation moved by 1% of the time
where the time goes in v7:
time: 270 us; the launch traced here: 269 us
  Pallas kernels  269 us (100%)
    pallas_call x1, Pallas kernels, body(): pl.pallas_call(kernel, out_shape=tuple((pltpu.VMEM(sh.shape, BF16) for sh...  266 us

profile of v7, /device:TPU:1, one launch (start us, length us, event | category | flops | bytes accessed | tf_op | source)
XLA Modules:
  0.0 269.3 jit_solution(3321411419730461825)
XLA Ops:
  0.6 265.8 %shard_map.121 = (bf16[32,128,128]{2,1,0:T(8,128)(2,1)S(1)}, bf16[32,128,128]{2,1,0:T(8,128)(2,1)S(1)}, bf16[1,32,128,512]{3,2,1,0:T(8,128)(2,1)S(1)}) custom-call(bf16[1,32,128,512]{3,2,1,0:T(8,128)(2,1)} %buf_ref.1, bf16[32,128,512]{2,1,0:T(8,128)(2,1)} %mb_ref.1, s32[1,512]{1,0:T(1,128)} %bitcast.1, f32[1,128]{1,0:T(1,128)} %constant.2.clone.freq_ref, ...), custom_call_target="tpu_custom_call" | custom-call | flops 60000002048 | bytes 40000000 | tf_op jit(solution)/shard_map/pallas_call | solution.py:344
  266.4 2.7 %shard_map.122 = (bf16[32,128,128]{2,1,0:T(8,128)(2,1)}, bf16[32,128,128]{2,1,0:T(8,128)(2,1)}, bf16[1,32,128,512]{3,2,1,0:T(8,128)(2,1)}) custom-call(bf16[32,128,128]{2,1,0:T(8,128)(2,1)S(1)} %get-tuple-element.6.refs_0_, bf16[32,128,128]{2,1,0:T(8,128)(2,1)S(1)} %get-tuple-element.7.refs_1_, bf16[1,32,128,512]{3,2,1,0:T(8,128)(2,1)S(1)} %get-tuple-element.8.refs_2_), custom_call_target="tpu_custom_call" | custom-call | flops 1000000 | bytes 12000000 | tf_op jit(solution)/shard_map/pallas_call | solution.py:371
